TPU v7x, 256 devices: a whole 4x4x8 slice. The times are simulated.
256 devices in a mesh: tile: 64 (over y, z, core), row: 4 (over x).
Axes of the slice: x: 4, y: 4, z: 8, core: 2. Of those that a mesh axis runs over, the one named last changes fastest.
Arguments:
- intensity: bfloat16 [64, 128, 11264], P('tile', 'row'), may hold values from 0.099609375 to 1
- volume: float32 [512, 128, 256], P('tile', 'row'), may hold values from 0 to 1
- footprint: bfloat16 [64, 256, 256], P('tile'), may hold values from 0.0001335144 to 0.0026855469
- foot_offset: int32 [512, 64], replicated, may hold values from 2 to 84, as said below
- tile_count: int32 [64], replicated, may hold values from 1 to 8, as said below
Outputs:
- residual: float32 [64, 128, 11264], P('tile', 'row')
- correction: float32 [512, 128, 256], P('tile', 'row')
Inputs may be any that keep to these rules, and one draw needn't show every extreme that they name: `foot_offset`: slot j belongs to group j // 8. At every angle the offsets of one group's slots differ by at most 3; wherever a group has two or more slots, by exactly 3. `tile_count`: some group has all its slots live.
All inputs are finite; a program needn't handle non-finite values.
Results may differ from a plain program's by a relative error of at most 0.00065.
Values may be sent and summed in bfloat16 or wider, within the bound.
A program may use at most 128 MiB of HBM per device.

v0:
```python
import jax
import jax.numpy as jnp
import numpy as np
from jax import lax
from jax.sharding import PartitionSpec as P

RIM = 3


decay_length = 2.0
row_floor = 0.5


def with_halo(block, sides, width):
    for axis, dim in sides:
        count = lax.axis_size(axis)
        forward = [(i, i + 1) for i in range(count - 1)]
        backward = [(target, source) for source, target in forward]
        low = lax.ppermute(
            lax.slice_in_dim(block, block.shape[dim] - width, None, axis=dim), axis, forward
        )
        high = lax.ppermute(lax.slice_in_dim(block, 0, width, axis=dim), axis, backward)
        block = jnp.concatenate([low, block, high], axis=dim)
    return block


def over_pieces(x, axis):
    tiles = lax.all_gather(x, axis)
    return tiles.sum(axis=0)


def smoothing_taps():
    spread_taps = np.exp(-np.abs(np.arange(-RIM, RIM + 1)) / decay_length)
    return spread_taps / spread_taps.sum()


def retrieve_phase(intensity):
    padded = with_halo(intensity, (("row", 1),), RIM)
    tap_weights = smoothing_taps()
    height_rows = intensity.shape[1]
    column_count = intensity.shape[2]
    across = float(tap_weights[0]) * padded[:, 0:height_rows, :].astype(jnp.float32)
    for tap_index in range(1, 2 * RIM + 1):
        across = across + float(tap_weights[tap_index]) * padded[
            :, tap_index : tap_index + height_rows, :
        ].astype(jnp.float32)
    widened = jnp.pad(across, ((0, 0), (0, 0), (RIM, RIM)))
    smoothed = float(tap_weights[0]) * widened[:, :, 0:column_count]
    for tap_index in range(1, 2 * RIM + 1):
        smoothed = (
            smoothed
            + float(tap_weights[tap_index]) * widened[:, :, tap_index : tap_index + column_count]
        )
    return -jnp.log(smoothed)


def live_flags(tile_count, slots_here):
    group_total = tile_count.shape[0]
    slot_ids = jnp.arange(group_total * slots_here, dtype=jnp.int32)
    repeated = jnp.broadcast_to(tile_count[:, None], (group_total, slots_here)).reshape(-1)
    return (slot_ids % slots_here < repeated).astype(jnp.float32)


def row_totals(footprint, offsets_here, live_all, block_count):
    half_cols = footprint.shape[2] // 2
    block_ids = jnp.arange(block_count, dtype=jnp.int32)
    matches = (offsets_here[:, :, None] == block_ids[None, None, :]).astype(jnp.float32)
    counts = jnp.sum(matches * live_all[:, None, None], axis=0)
    voxel_sums = jnp.sum(footprint, axis=1, dtype=jnp.float32)
    leading = counts[:, :, None] * voxel_sums[:, None, :half_cols]
    trailing = counts[:, :, None] * voxel_sums[:, None, half_cols:]
    trailing = jnp.concatenate([jnp.zeros_like(trailing[:, :1]), trailing[:, :-1]], axis=1)
    return (leading + trailing).reshape(counts.shape[0], -1)


def project_loads(load_half, footprint):
    half_cols = footprint.shape[2] // 2
    images = jnp.einsum("abrv,avc->arbc", load_half, footprint, preferred_element_type=jnp.float32)
    leading = images[..., :half_cols]
    trailing = images[..., half_cols:]
    trailing = jnp.concatenate([jnp.zeros_like(trailing[:, :, :1]), trailing[:, :, :-1]], axis=2)
    joined = leading + trailing
    return joined.reshape(joined.shape[0], joined.shape[1], -1)


def back_project(weighted, footprint):
    half_cols = footprint.shape[2] // 2
    halves = weighted.reshape(weighted.shape[0], weighted.shape[1], -1, half_cols)
    nearer = jnp.einsum(
        "arbc,avc->abrv", halves, footprint[:, :, :half_cols], preferred_element_type=jnp.float32
    )
    farther = jnp.einsum(
        "arbc,avc->abrv", halves, footprint[:, :, half_cols:], preferred_element_type=jnp.float32
    )
    farther = jnp.concatenate([farther[:, 1:], jnp.zeros_like(farther[:, :1])], axis=1)
    return nearer + farther


def local(intensity, volume, footprint, foot_offset, tile_count):
    phase_map = retrieve_phase(intensity)
    slots_here = volume.shape[0]
    angles_here = footprint.shape[0]
    half_cols = footprint.shape[2] // 2
    block_count = intensity.shape[2] // half_cols
    member = lax.axis_index("tile")
    live_all = live_flags(tile_count, slots_here)
    live_mine = lax.dynamic_slice_in_dim(live_all, member * slots_here, slots_here)
    masked = volume * live_mine[:, None, None]
    offsets_here = lax.dynamic_slice_in_dim(foot_offset, member * angles_here, angles_here, 1)
    column_sums = over_pieces(jnp.sum(footprint, axis=(0, 2), dtype=jnp.float32), "tile")
    row_sums = row_totals(footprint, offsets_here, live_all, block_count)
    gathered = lax.all_gather(masked.astype(jnp.bfloat16), "tile", axis=0, tiled=True).astype(
        masked.dtype
    )
    load_blocks = jnp.stack(
        [jax.ops.segment_sum(gathered, offsets_here[:, 0], num_segments=block_count)]
    )
    projection = project_loads(load_blocks.astype(jnp.bfloat16), footprint)
    residual = phase_map - projection
    weighted = (residual / jnp.maximum(row_sums, row_floor)[:, None, :]).astype(jnp.bfloat16)
    back_blocks = back_project(weighted, footprint)
    slot_terms = jnp.take(back_blocks[0], offsets_here[:, 0], axis=0)
    summed = lax.psum_scatter(slot_terms, "tile", scatter_dimension=0, tiled=True)
    correction = summed * live_mine[:, None, None] / column_sums[None, None, :]
    return (residual, correction)


def solution(mesh):
    placed = (P("tile", "row", None), P("tile", "row", None), P("tile", None, None), P(), P())
    return jax.shard_map(
        local,
        mesh=mesh,
        in_specs=placed,
        out_specs=(P("tile", "row", None), P("tile", "row", None)),
        check_vma=False,
    )
```

profile of v0, /device:TPU:2, one launch (start us, length us, event | category | flops | bytes accessed | tf_op | source)
XLA Modules:
  0.0 383.2 jit_solution(14026764378721223923)
XLA Ops:
  7.2 0.8 broadcast_in_dim.12
  8.2 1.7 multiply_convert_fusion
  10.0 1.1 fusion.18
  11.0 4.2 %collective-permute-start.1 = (bf16[1,3,11264]{2,1,0:T(4,128)(2,1)S(1)}, bf16[1,3,11264]{2,1,0:T(4,128)(2,1)S(1)}, u32[]{:S(2)}, u32[]{:S(2)}) collective-permute-start(bf16[1,3,11264]{2,1,0:T(4,128)(2,1)S(1)} %get-tuple-element.19), channel_id=1, source_target_pairs={{1,0},{2,1},{3,2},{5,4},{6,5},{7,6},{9,8},{10,9},{11,10},{13,12},{... | collective-permute-start | bytes 202760 | tf_op jit(solution)/shard_map/ppermute | solution.py:22
  15.2 1.9 collective-permute-start
  17.1 0.8 and_reduce_fusion
  18.0 1.0 convert_reduce_fusion
  19.4 2.3 collective-permute-done
  21.6 2.5 multiply_add_fusion
  24.1 73.2 %all-gather.4.cloned.1.call-done = bf16[512,32,256]{2,1,0:T(8,128)(2,1)} async-done(((bf16[8,32,256]{2,1,0:T(8,128)(2,1)}), bf16[512,32,256]{2,1,0:T(8,128)(2,1)}) %all-gather.4.cloned.1.call-update) | async-done | bytes 8388624 | tf_op jit(solution)/shard_map/all_gather | solution.py:112
  97.3 11.3 %convert_element_type.57 = f32[512,32,256]{2,1,0:T(8,128)} convert(bf16[512,32,256]{2,1,0:T(8,128)(2,1)} %all-gather.4.cloned.1.call-done) | non-fusion elementwise | flops 4194304 | bytes 25165824 | tf_op jit(solution)/shard_map/convert_element_type | solution.py:112
  109.0 52.1 %scatter_fusion = f32[88,32,256]{2,1,0:T(8,128)S(1)} fusion(f32[88,32,256]{2,1,0:T(8,128)S(1)} %broadcast_in_dim.11, s32[512]{0:T(512)S(1)} %bitcast.56, f32[512,32,256]{2,1,0:T(8,128)} %convert_element_type.57), kind=kCustom, calls=%fused_computation.1 | custom fusion | flops 4194304 | bytes 50333696 | tf_op jit(solution)/shard_map/scatter-add | solution.py:116
  161.1 0.5 convolution_bitcast_fusion.1
  162.0 0.8 copy.41
  162.8 0.5 copy-done
  163.3 3.4 fusion.7
  166.9 0.6 convolution_bitcast_fusion
  167.6 0.6 fusion
  168.2 0.9 copy.43
  169.2 7.0 %gather_fusion = f32[512,32,256]{2,1,0:T(8,128)} fusion(f32[88,32,256]{2,1,0:T(8,128)S(1)} %copy.43, s32[1024]{0:T(1024)S(1)} %pad_clamp_fusion), kind=kCustom, calls=%fused_computation | custom fusion | bytes 33556480 | tf_op jit(solution)/shard_map/jit(_take)/gather | solution.py:122
  176.1 11.7 %broadcast_select_fusion = f32[512,32,256]{2,1,0:T(8,128)} fusion(f32[512,32,256]{2,1,0:T(8,128)} %gather_fusion, pred[512]{0:T(512)(128)(4,1)S(1)} %get-tuple-element.14), kind=kLoop, calls=%fused_computation.2 | loop fusion | flops 4194304 | bytes 33554944 | tf_op jit(solution)/shard_map/jit(_take)/select_n | solution.py:122
  187.9 42.4 %all-gather.1 = f32[64,1,256]{2,1,0:T(1,128)S(1)} all-gather(f32[1,1,256]{2,1,0:T(1,128)S(1)} %bitcast.59), channel_id=2, replica_groups=mesh['tile'=64,'row'=4] {'tile'}, dimensions={0}, use_global_device_ids=true | all-gather | bytes 66560 | tf_op jit(solution)/shard_map/all_gather | solution.py:28
  230.4 144.3 %reduce-scatter.2.cloned.1.call-done = f32[8,32,256]{2,1,0:T(8,128)} async-done(((f32[512,32,256]{2,1,0:T(8,128)}), f32[8,32,256]{2,1,0:T(8,128)}) %reduce-scatter.2.cloned.1.call-update) | async-done | bytes 262160 | tf_op jit(solution)/shard_map/reduce_scatter | solution.py:123
  374.7 1.7 multiply_divide_fusion
  (26 shorter events, 1.8 us)
Async XLA Ops:
  7.2 12.0 %copy-start.1 = (bf16[1,32,11264]{2,1,0:T(8,128)(2,1)S(1)}, bf16[1,32,11264]{2,1,0:T(8,128)(2,1)}, u32[]{:S(2)}) copy-start(bf16[1,32,11264]{2,1,0:T(8,128)(2,1)} %param.5) | copy-start | bytes 2162692
  7.2 90.1 %all-gather.4.cloned.1.call-start = ((), (), s32[]{:S(2)}) async-start(), calls=%async_computation.1 | async-start | bytes 8519680 | tf_op jit(solution)/shard_map/all_gather | solution.py:112
  9.9 364.7 %reduce-scatter.2.cloned.1.call-start = ((), (), s32[]{:S(2)}) async-start(), calls=%async_computation.2 | async-start | bytes 17039360 | tf_op jit(solution)/shard_map/reduce_scatter | solution.py:123
  11.0 8.2 %collective-permute-start.1 = (bf16[1,3,11264]{2,1,0:T(4,128)(2,1)S(1)}, bf16[1,3,11264]{2,1,0:T(4,128)(2,1)S(1)}, u32[]{:S(2)}, u32[]{:S(2)}) collective-permute-start(bf16[1,3,11264]{2,1,0:T(4,128)(2,1)S(1)} %get-tuple-element.19), channel_id=1, source_target_pairs={{1,0},{2,1},{3,2},{5,4},{6,5},{7,6},{9,8},{10,9},{11,10},{13,12},{... | collective-permute-start | bytes 202760 | tf_op jit(solution)/shard_map/ppermute | solution.py:22
  15.2 6.4 %collective-permute-start = (bf16[1,3,11264]{2,1,0:T(4,128)(2,1)S(1)}, bf16[1,3,11264]{2,1,0:T(4,128)(2,1)S(1)}, u32[]{:S(2)}, u32[]{:S(2)}) collective-permute-start(bf16[1,3,11264]{2,1,0:T(4,128)(2,1)S(1)} %get-tuple-element.20), channel_id=1, source_target_pairs={{0,1},{1,2},{2,3},{4,5},{5,6},{6,7},{8,9},{9,10},{10,11},{12,13},{... | collective-permute-start | bytes 202760 | tf_op jit(solution)/shard_map/ppermute | solution.py:19
  109.0 52.1 %copy-start.2 = (bf16[1,256,256]{2,1,0:T(8,128)(2,1)S(1)}, bf16[1,256,256]{2,1,0:T(8,128)(2,1)}, u32[]{:S(2)}) copy-start(bf16[1,256,256]{2,1,0:T(8,128)(2,1)} %param.7) | copy-start | bytes 393220
  162.0 1.4 copy-start
Sparse Core Ops, SparseCore 0:
  11.3 85.9 all-gather.3
  188.0 186.6 reduce-scatter.1
where the time goes:
time: 385 us; the launch traced here: 383 us
  waiting for transfers between devices  220 us (57%)
  other arithmetic  86.7 us (23%)
  blocking collectives  42.4 us (11%)
  between operations  14.2 us (4%)
  local copies, waits for them, and re-layouts  12.2 us (3%)
  starting transfers between devices  6.15 us (2%)
    reduce_scatter x1, waiting for transfers between devices, local(): lax.psum_scatter(slot_terms, 'tile', scatter_dimension=0, tiled=True)  144 us
    all_gather x1, waiting for transfers between devices, local(): lax.all_gather(masked.astype(jnp.bfloat16), 'tile', axis=0, tiled=True)  73.2 us
    scatter-add x1, other arithmetic, local(): jax.ops.segment_sum(gathered, offsets_here[:, 0], num_segments=block_count)  52.1 us
    all_gather x1, blocking collectives, over_pieces(): tiles = lax.all_gather(x, axis)  42.4 us
    select_n x1, other arithmetic, local(): slot_terms = jnp.take(back_blocks[0], offsets_here[:, 0], axis=0)  11.7 us
    convert_element_type x1, other arithmetic, local(): lax.all_gather(masked.astype(jnp.bfloat16), 'tile', axis=0, tiled=True)  11.3 us
  transfers between devices with their start and end apart: 4, of which 3 were waited for; matrix products, arithmetic and copies ran while one was open for 2% of the time, Pallas kernels for 0%

commit v1 on v0

v1 whole, which is shorter than its diff:
```python
import functools

import jax
import jax.numpy as jnp
import numpy as np
from jax import lax
from jax.experimental import pallas as pl
from jax.experimental.pallas import tpu as pltpu
from jax.sharding import PartitionSpec as P

RIM = 3
NCB = 88
CB = 128
TV = 256
YS, ZS, CS, XS = 4, 8, 2, 4
SLOTS = 8
RB = 8
SUB = RB * TV
TOTAL = YS * ZS * CS * SLOTS
BP = 96
ROWS_HERE = YS * RB

decay_length = 2.0
row_floor = 0.5

F32 = jnp.float32
BF16 = jnp.bfloat16
MESH = pl.DeviceIdType.MESH


def smoothing_taps():
    spread_taps = np.exp(-np.abs(np.arange(-RIM, RIM + 1)) / decay_length)
    return [float(t) for t in (spread_taps / spread_taps.sum()).astype(np.float32)]


def dot(a, b, dims=((1,), (0,))):
    return lax.dot_general(a, b, (dims, ((), ())), preferred_element_type=F32)


def kernel(
    inten, vol, foot, offm, offmt,
    res_out, cor_out, col_out,
    vol_s, vol_g, foot_g, cs_y, cs_g,
    halo_lo, halo_hi, rows_p, rows_a, ph_s, ph,
    hot, hot_t, loads, weigh, res_w, back, terms, pair_r, ring_r,
    y_send, y_recv, h_send, h_recv, g_send, g_recv, q_send, q_recv,
    p_send, p_recv, r_send, r_recv, l_sem,
):
    taps = smoothing_taps()
    t = lax.axis_index("tile")
    x = lax.axis_index("row")
    y = t // (ZS * CS)
    zc = t % (ZS * CS)
    z = zc // CS
    c = zc % CS

    def tile_of(yy, zz, cc):
        return (yy * ZS + zz) * CS + cc

    def device(yy, zz, cc):
        return (tile_of(yy, zz, cc), x)

    partner = device(y, z, 1 - c)
    right = device(y, (z + 1) % ZS, c)
    left = device(y, (z + ZS - 1) % ZS, c)
    toward = (right, left)
    y_peer = [(y + d) % YS for d in range(1, YS)]
    y_from = [(y + YS - d) % YS for d in range(1, YS)]
    x_up = (t, (x + 1) % XS)
    x_down = (t, (x + XS - 1) % XS)

    barrier = pltpu.get_barrier_semaphore()
    peers = [device(yy, z, c) for yy in y_peer] + [partner, right, left, x_up, x_down]
    for peer in peers:
        pl.semaphore_signal(barrier, inc=1, device_id=peer, device_id_type=MESH)
    pl.semaphore_wait(barrier, len(peers))

    started = []

    def send(src, dst, ssem, rsem, dev):
        copy = pltpu.make_async_remote_copy(
            src_ref=src, dst_ref=dst, send_sem=ssem, recv_sem=rsem,
            device_id=dev, device_id_type=MESH,
        )
        copy.start()
        started.append(copy)

    def arrive(dst, ssem, rsem, dev):
        pltpu.make_async_remote_copy(
            src_ref=dst, dst_ref=dst, send_sem=ssem, recv_sem=rsem,
            device_id=dev, device_id_type=MESH,
        ).wait_recv()

    def y_copy(kind, d, src, dst):
        send(src, dst, y_send.at[kind, d], y_recv.at[kind, d], device(y_peer[d], z, c))

    def y_wait(kind, d, dst):
        arrive(dst, y_send.at[kind, d], y_recv.at[kind, d], device(y_from[d], z, c))

    send(inten.at[0, pl.ds(ROWS_HERE - 8, 8), :], halo_lo, h_send.at[0], h_recv.at[0], x_up)
    send(inten.at[0, pl.ds(0, 8), :], halo_hi, h_send.at[1], h_recv.at[1], x_down)

    for q in range(YS):
        for r in range(RB):
            vol_s[q, :, r * TV : (r + 1) * TV] = vol[:, q * RB + r, :].astype(BF16)
    for d in range(3):
        y_copy(0, d, vol_s.at[y_peer[d]], vol_g.at[y, zc])
    ones = jnp.ones((8, TV), BF16)
    cs_y[y] = dot(ones, foot[0], ((1,), (1,)))
    for d in range(3):
        y_copy(1, d, cs_y.at[y], cs_y.at[y])
    for d in range(3):
        y_copy(2, d, foot.at[0], foot_g.at[y])
    vol_g[y, zc] = vol_s[y]
    foot_g[y] = foot[0]

    def chunk_of(zz, cc, p):
        return vol_g.at[pl.ds(2 * p, 2), zz * CS + cc]

    def give_partner(index, zz, p):
        src = chunk_of(zz, c, p)
        send(src, src, q_send.at[index, p], q_recv.at[index, p], partner)

    def give_partner_sums(index, zz):
        src = cs_g.at[zz * CS + c]
        send(src, src, q_send.at[index, 2], q_recv.at[index, 2], partner)

    def ring_send(way, step, p, zz):
        src = chunk_of(zz, c, p)
        send(src, src, g_send.at[way, step, p], g_recv.at[way, step, p], toward[way])

    def ring_wait(way, step, p, zz):
        arrive(chunk_of(zz, c, p), g_send.at[way, step, p], g_recv.at[way, step, p], toward[1 - way])

    def sums_send(way, step, zz):
        src = cs_g.at[zz * CS + c]
        send(src, src, g_send.at[way, step, 2], g_recv.at[way, step, 2], toward[way])

    def sums_wait(way, step, zz):
        arrive(cs_g.at[zz * CS + c], g_send.at[way, step, 2], g_recv.at[way, step, 2], toward[1 - way])

    for d in range(3):
        y_wait(0, d, vol_g.at[y_from[d], zc])
    for p in range(2):
        for way in range(2):
            ring_send(way, 0, p, z)
    for d in range(3):
        y_wait(1, d, cs_y.at[y_from[d]])
    cs_g[zc] = cs_y[0] + cs_y[1] + cs_y[2] + cs_y[3]
    for way in range(2):
        sums_send(way, 0, z)
    for p in range(2):
        give_partner(0, z, p)
    give_partner_sums(0, z)

    arrive(halo_lo, h_send.at[0], h_recv.at[0], x_down)
    arrive(halo_hi, h_send.at[1], h_recv.at[1], x_up)
    rows_a[0] = jnp.zeros((ROWS_HERE, CB), F32)
    rows_a[NCB + 1] = jnp.zeros((ROWS_HERE, CB), F32)
    has_lo = (x > 0).astype(F32)
    has_hi = (x < XS - 1).astype(F32)

    def vertical(b, _):
        cols = pl.ds(pl.multiple_of(b * CB, CB), CB)
        rows_p[b, 0:8, :] = halo_lo[:, cols].astype(F32) * has_lo
        rows_p[b, 8 : 8 + ROWS_HERE, :] = inten[0, :, cols].astype(F32)
        rows_p[b, 8 + ROWS_HERE : 16 + ROWS_HERE, :] = halo_hi[:, cols].astype(F32) * has_hi
        across = taps[RIM] * rows_p[b, 8 : 8 + ROWS_HERE, :]
        for k in range(1, RIM + 1):
            across = across + taps[RIM + k] * (
                rows_p[b, 8 - k : 8 - k + ROWS_HERE, :] + rows_p[b, 8 + k : 8 + k + ROWS_HERE, :]
            )
        rows_a[b + 1] = across
        return 0

    lax.fori_loop(0, NCB, vertical, 0)
    lane = lax.broadcasted_iota(jnp.int32, (ROWS_HERE, CB), 1)

    def horizontal(b, _):
        before, here, after = rows_a[b], rows_a[b + 1], rows_a[b + 2]
        smooth = taps[RIM] * here
        for k in range(1, RIM + 1):
            ahead = pltpu.roll(jnp.where(lane < k, after, here), CB - k, 1)
            behind = pltpu.roll(jnp.where(lane >= CB - k, before, here), k, 1)
            smooth = smooth + taps[RIM + k] * (ahead + behind)
        phase = -jnp.log(smooth)
        for q in range(YS):
            ph_s[q, pl.ds(pl.multiple_of(b * RB, RB), RB), :] = phase[q * RB : (q + 1) * RB]
        return 0

    lax.fori_loop(0, NCB, horizontal, 0)
    for d in range(3):
        y_copy(3, d, ph_s.at[y_peer[d]], ph.at[y])
    ph[y] = ph_s[y]

    for step in range(1, 5):
        for p in range(2):
            for way in range(2):
                if step == 4 and p != way:
                    continue
                zz = (z + ZS - step) % ZS if way == 0 else (z + step) % ZS
                ring_wait(way, step - 1, p, zz)
                if step < 3 or (step == 3 and p == way):
                    ring_send(way, step, p, zz)
                index = step if way == 0 or step == 4 else 4 + step
                give_partner(index, zz, p)
        for way in range(2):
            if step == 4 and way == 1:
                continue
            zz = (z + ZS - step) % ZS if way == 0 else (z + step) % ZS
            sums_wait(way, step - 1, zz)
            if step < 3 or (step == 3 and way == 0):
                sums_send(way, step, zz)
            give_partner_sums(step if way == 0 else 4 + step, zz)

    block = lax.broadcasted_iota(jnp.int32, (BP, TOTAL), 0)
    for i in range(YS):
        row = offmt[pl.ds(tile_of(i, z, c), 1), :]
        hot[i * BP : (i + 1) * BP, :] = (row == block).astype(F32).astype(BF16)
    angle = lax.broadcasted_iota(jnp.int32, (TOTAL, YS * ZS * CS), 1)
    block_t = lax.broadcasted_iota(jnp.int32, (TOTAL, CB), 1)
    for i in range(YS):
        col = jnp.sum(jnp.where(angle == tile_of(i, z, c), offm[...], 0), axis=1, keepdims=True)
        hot_t[:, i * CB : (i + 1) * CB] = (col == block_t).astype(F32).astype(BF16)
    for h in range(2):
        for i in range(YS):
            back[h, i * CB + BP : (i + 1) * CB, :] = jnp.zeros((CB - BP, SUB), BF16)

    for d in range(3):
        y_wait(2, d, foot_g.at[y_from[d]])
    for index in range(8):
        zz = (z + ZS - index) % ZS if index < 5 else (z + index - 4) % ZS
        for p in range(2):
            arrive(chunk_of(zz, 1 - c, p), q_send.at[index, p], q_recv.at[index, p], partner)
        arrive(cs_g.at[zz * CS + 1 - c], q_send.at[index, 2], q_recv.at[index, 2], partner)

    def load_row(r, _):
        cols = pl.ds(pl.multiple_of(r * TV, TV), TV)
        got = dot(hot[...], vol_g[:, :, :, cols].reshape(TOTAL, TV)).astype(BF16)
        for i in range(YS):
            loads[i, pl.ds(pl.multiple_of(r * BP, BP), BP), :] = got[i * BP : (i + 1) * BP]
        return 0

    lax.fori_loop(0, RB, load_row, 0)
    for d in range(3):
        y_wait(3, d, ph.at[y_from[d]])

    def one_angle(i, _):
        table = foot_g[i]
        counts = jnp.sum(hot[pl.ds(pl.multiple_of(i * BP, BP), BP), :].astype(F32), axis=1, keepdims=True)
        sums = dot(ones, table)[0:1]
        totals = counts * sums[:, :CB] + pltpu.roll(counts * sums[:, CB:], 1, 0)
        scale = (1.0 / jnp.maximum(totals, row_floor))[:NCB]
        images = dot(loads[i], table)
        for r in range(RB):
            image = images[r * BP : (r + 1) * BP]
            shadow = image[:, :CB] + pltpu.roll(image[:, CB:], 1, 0)
            left_over = ph[i, pl.ds(r, NCB, stride=RB), :] - shadow[:NCB]
            res_w[i, pl.ds(r, NCB, stride=RB), :] = left_over
            near = jnp.concatenate([left_over * scale, jnp.zeros((BP - NCB, CB), F32)], axis=0)
            far = pltpu.roll(near, BP - 1, 0)
            weigh[r * BP : (r + 1) * BP, :] = jnp.concatenate([near, far], axis=1).astype(BF16)
        spread = dot(weigh[...], table, ((1,), (1,)))
        rows = pl.ds(pl.multiple_of(i * CB, CB), BP)
        for r in range(RB):
            part = spread[r * BP : (r + 1) * BP]
            high = part.astype(BF16)
            back[0, rows, r * TV : (r + 1) * TV] = high
            back[1, rows, r * TV : (r + 1) * TV] = (part - high.astype(F32)).astype(BF16)
        return 0

    lax.fori_loop(0, YS, one_angle, 0)
    for d in range(3):
        y_copy(4, d, res_w.at[y_peer[d]], res_out.at[y])
    own_res = pltpu.make_async_copy(res_w.at[y], res_out.at[y], l_sem.at[0])
    own_res.start()

    def term_row(r, _):
        cols = pl.ds(pl.multiple_of(r * TV, TV), TV)
        got = dot(hot_t[...], back[0, :, cols]) + dot(hot_t[...], back[1, :, cols])
        terms[:, :, :, :, cols] = got.reshape(YS, ZS, CS, SLOTS, TV)
        return 0

    lax.fori_loop(0, RB, term_row, 0)

    order = (4, 3, 5, 2, 6, 1, 7, 0)
    for off in order:
        zz = (z + off) % ZS
        send(terms.at[:, zz, 1 - c], pair_r.at[zz], p_send.at[off], p_recv.at[off], partner)

    def add_pair(off):
        zz = (z + off) % ZS
        arrive(pair_r.at[zz], p_send.at[off], p_recv.at[off], partner)
        terms[:, zz, c] = terms[:, zz, c] + pair_r[zz]

    def sum_send(way, step, p, zz):
        send(
            terms.at[pl.ds(2 * p, 2), zz, c], ring_r.at[way, step, p],
            r_send.at[way, step, p], r_recv.at[way, step, p], toward[way],
        )

    def sum_wait(way, step, p):
        arrive(ring_r.at[way, step, p], r_send.at[way, step, p], r_recv.at[way, step, p], toward[1 - way])

    for step in range(4):
        for way in range(2):
            if step > 0 or way == 0:
                add_pair(4 - step if way == 0 else 4 + step)
        for p in range(2):
            for way in range(2):
                if step == 0 and p != way:
                    continue
                zz = (z + 4 - step) % ZS if way == 0 else (z + 4 + step) % ZS
                if step > 1 or (step == 1 and p == way):
                    sum_wait(way, step - 1, p)
                    half = pl.ds(2 * p, 2)
                    terms[half, zz, c] = terms[half, zz, c] + ring_r[way, step - 1, p]
                sum_send(way, step, p, zz)
    add_pair(0)
    for p in range(2):
        half = pl.ds(2 * p, 2)
        for way in range(2):
            sum_wait(way, 3, p)
            terms[half, z, c] = terms[half, z, c] + ring_r[way, 3, p]
    for d in range(3):
        y_copy(5, d, terms.at[y_peer[d], z, c], cor_out.at[y])
    own_cor = pltpu.make_async_copy(terms.at[y, z, c], cor_out.at[y], l_sem.at[1])
    own_cor.start()
    total = cs_g[0]
    for k in range(1, ZS * CS):
        total = total + cs_g[k]
    col_out[...] = total

    for d in range(3):
        y_wait(4, d, res_out.at[y_from[d]])
    for d in range(3):
        y_wait(5, d, cor_out.at[y_from[d]])
    own_res.wait()
    own_cor.wait()
    for copy in started:
        copy.wait_send()


def local(intensity, volume, footprint, foot_offset, tile_count):
    live = (jnp.arange(SLOTS, dtype=jnp.int32)[None, :] < tile_count[:, None]).reshape(TOTAL, 1)
    masked = jnp.where(live, foot_offset, -1)
    dma = pltpu.SemaphoreType.DMA
    vmem = pl.BlockSpec(memory_space=pltpu.VMEM)
    hbm = pl.BlockSpec(memory_space=pl.ANY)
    residual, summed, columns = pl.pallas_call(
        kernel,
        out_shape=(
            jax.ShapeDtypeStruct((YS, NCB * RB, CB), F32),
            jax.ShapeDtypeStruct((YS, SLOTS, SUB), F32),
            jax.ShapeDtypeStruct((8, TV), F32),
        ),
        in_specs=[vmem] * 5,
        out_specs=(hbm, hbm, vmem),
        scratch_shapes=[
            pltpu.VMEM((YS, SLOTS, SUB), BF16),
            pltpu.VMEM((YS, ZS * CS, SLOTS, SUB), BF16),
            pltpu.VMEM((YS, TV, TV), BF16),
            pltpu.VMEM((YS, 8, TV), F32),
            pltpu.VMEM((ZS * CS, 8, TV), F32),
            pltpu.VMEM((8, NCB * CB), BF16),
            pltpu.VMEM((8, NCB * CB), BF16),
            pltpu.VMEM((NCB, ROWS_HERE + 16, CB), F32),
            pltpu.VMEM((NCB + 2, ROWS_HERE, CB), F32),
            pltpu.VMEM((YS, NCB * RB, CB), F32),
            pltpu.VMEM((YS, NCB * RB, CB), F32),
            pltpu.VMEM((YS * BP, TOTAL), BF16),
            pltpu.VMEM((TOTAL, YS * CB), BF16),
            pltpu.VMEM((YS, RB * BP, TV), BF16),
            pltpu.VMEM((RB * BP, TV), BF16),
            pltpu.VMEM((YS, NCB * RB, CB), F32),
            pltpu.VMEM((2, YS * CB, SUB), BF16),
            pltpu.VMEM((YS, ZS, CS, SLOTS, SUB), F32),
            pltpu.VMEM((ZS, YS, SLOTS, SUB), F32),
            pltpu.VMEM((2, 4, 2, 2, SLOTS, SUB), F32),
            dma((6, 3)), dma((6, 3)),
            dma((2,)), dma((2,)),
            dma((2, 4, 3)), dma((2, 4, 3)),
            dma((8, 3)), dma((8, 3)),
            dma((8,)), dma((8,)),
            dma((2, 4, 2)), dma((2, 4, 2)),
            dma((2,)),
        ],
        compiler_params=pltpu.CompilerParams(
            collective_id=0, has_side_effects=True, vmem_limit_bytes=60 << 20
        ),
        name="sirt",
    )(intensity, volume, footprint, masked, masked.T)
    residual = (
        residual.reshape(YS, NCB, RB, CB).transpose(0, 2, 1, 3).reshape(1, ROWS_HERE, NCB * CB)
    )
    summed = summed.reshape(YS, SLOTS, RB, TV).transpose(1, 0, 2, 3).reshape(SLOTS, ROWS_HERE, TV)
    return residual, summed / columns[0][None, None, :]


def solution(mesh):
    placed = (P("tile", "row", None), P("tile", "row", None), P("tile", None, None), P(), P())
    return jax.shard_map(
        local,
        mesh=mesh,
        in_specs=placed,
        out_specs=(P("tile", "row", None), P("tile", "row", None)),
        check_vma=False,
    )
```

time: 385 us -> 92.8 us (0.24)
  waiting for transfers between devices: 220 us -> 0 us
  other arithmetic: 86.7 us -> 4.96 us
  Pallas kernels: 0 us -> 81.4 us
  blocking collectives: 42.4 us -> 0 us
  between operations: 14.2 us -> 0.65 us
  local copies, waits for them, and re-layouts: 12.2 us -> 4.18 us
  starting transfers between devices: 6.15 us -> 0 us
    reduce_scatter x1 -> x0, waiting for transfers between devices: 144 us -> none  [local(): lax.psum_scatter(slot_terms, 'tile', scatter_dimension=0, tiled=True)]
    pallas_call x0 -> x1, Pallas kernels: none -> 81.4 us  [local(): pl.pallas_call(kernel, out_shape=(jax.ShapeDtypeStruct((YS, NCB * RB, CB)...]
    all_gather x1 -> x0, waiting for transfers between devices: 73.2 us -> none  [local(): lax.all_gather(masked.astype(jnp.bfloat16), 'tile', axis=0, tiled=True)]
    scatter-add x1 -> x0, other arithmetic: 52.1 us -> none  [local(): jax.ops.segment_sum(gathered, offsets_here[:, 0], num_segments=block_count)]
    all_gather x1 -> x0, blocking collectives: 42.4 us -> none  [over_pieces(): tiles = lax.all_gather(x, axis)]
    convert_element_type x3 -> x0, other arithmetic: 13 us -> none  [the longest x1 11.3 us: local(): lax.all_gather(masked.astype(jnp.bfloat16), 'tile', axis=0, tiled=True)]
    select_n x1, other arithmetic: 11.7 us -> 0.92 us  [local(): masked = jnp.where(live, foot_offset, -1)]
    gather x1 -> x0, local copies, waits for them, and re-layouts: 6.97 us -> none  [local(): slot_terms = jnp.take(back_blocks[0], offsets_here[:, 0], axis=0)]
  transfers between devices with their start and end apart: 4 -> 0, of which waited for: 3 -> 0; matrix products, arithmetic and copies ran while one was open for 2% -> 0% of each run, Pallas kernels for 0% -> 0%
where the time goes in v1:
time: 92.8 us; the launch traced here: 91.2 us
  Pallas kernels  81.4 us (88%)
  other arithmetic  4.96 us (5%)
  local copies, waits for them, and re-layouts  4.18 us (5%)
    pallas_call x1, Pallas kernels, local(): pl.pallas_call(kernel, out_shape=(jax.ShapeDtypeStruct((YS, NCB * RB, CB)...  81.4 us
    unnamed x1, local copies, waits for them, and re-layouts  2.55 us

profile of v1, /device:TPU:2, one launch (start us, length us, event | category | flops | bytes accessed | tf_op | source)
XLA Modules:
  0.0 91.2 jit_solution(155265457287026964)
XLA Ops:
  0.6 0.7 iota_compare_fusion
  1.4 0.1 lt.23
  1.5 0.9 %broadcast_select_fusion = s32[512,64]{0,1:T(8,128)S(1)} fusion(s32[512,64]{0,1:T(8,128)} %param.8, pred[512]{0:T(512)(128)(4,1)S(1)} %lt.23), kind=kLoop, calls=%fused_computation.1 | loop fusion | flops 32768 | bytes 262656 | tf_op jit(solution)/shard_map/jit(_where)/select_n | solution.py:346
  2.4 0.8 copy.9.offm
  3.2 1.6 %fusion.offmt = s32[64,512]{1,0:T(8,128)} fusion(s32[512,64]{0,1:T(8,128)} %param.8, pred[512]{0:T(512)(128)(4,1)S(1)} %lt.23), kind=kLoop, calls=%fused_computation.3 | loop fusion | flops 32768 | bytes 262656 | tf_op jit(solution)/shard_map/transpose | solution.py:392
  4.8 81.4 %sirt.1 = (f32[4,704,128]{2,1,0:T(8,128)}, f32[4,8,2048]{2,1,0:T(8,128)}, f32[8,256]{1,0:T(8,128)}) custom-call(bf16[1,32,11264]{2,1,0:T(8,128)(2,1)} %inten.1, f32[8,32,256]{2,1,0:T(8,128)} %vol.1, bf16[1,256,256]{2,1,0:T(8,128)(2,1)} %foot.1, s32[512,64]{1,0:T(8,128)} %copy.9.offm, s32[64,512]{1,0:T(8,128)} %fusion.offmt), custom_call_target="tpu_custom_call" | custom-call | tf_op jit(solution)/shard_map/sirt/pallas_call | solution.py:350
  86.2 0.7 slice.3
  86.9 1.7 %bitcast_divide_fusion = f32[8,32,256]{2,1,0:T(8,128)} fusion(f32[8,4,8,256]{3,0,2,1:T(8,128)} %bitcast.14, f32[256]{0:T(256)S(1)} %bitcast.15), kind=kLoop, calls=%fused_computation | loop fusion | flops 65536 | bytes 525312 | tf_op jit(solution)/shard_map/div | solution.py:397
  88.7 2.6 %copy.13 = f32[1,32,11264]{2,1,0:T(8,128)} copy(f32[1,32,11264]{2,1,0:T(8,128)} %bitcast.13) | data formatting | bytes 2883584

commit v2 on v1

v2 whole, which is shorter than its diff:
```python
import functools

import jax
import jax.numpy as jnp
import numpy as np
from jax import lax
from jax.experimental import pallas as pl
from jax.experimental.pallas import tpu as pltpu
from jax.sharding import PartitionSpec as P

RIM = 3
NCB = 88
CB = 128
TV = 256
YS, ZS, CS, XS = 4, 8, 2, 4
SLOTS = 8
RB = 8
SUB = RB * TV
TOTAL = YS * ZS * CS * SLOTS
BP = 96
PART = TV // XS
ROWS_HERE = YS * RB

decay_length = 2.0
row_floor = 0.5

F32 = jnp.float32
BF16 = jnp.bfloat16
MESH = pl.DeviceIdType.MESH


def smoothing_taps():
    spread_taps = np.exp(-np.abs(np.arange(-RIM, RIM + 1)) / decay_length)
    return [float(t) for t in (spread_taps / spread_taps.sum()).astype(np.float32)]


def dot(a, b, dims=((1,), (0,))):
    return lax.dot_general(a, b, (dims, ((), ())), preferred_element_type=F32)


def kernel(
    inten_h, vol, foot, off_t, count,
    res_out, cor_out, col_out,
    inten, vol_s, vol_g, foot_g, cs_y, cs_g,
    halo_lo, halo_hi, rows_p, rows_a, ph_s, ph,
    hot, hot_t, loads, images, weigh, res_w, back, terms, pair_r, ring_r, fin,
    y_send, y_recv, h_send, h_recv, x_send, x_recv, g_send, g_recv, c_send, c_recv,
    q_send, q_recv, p_send, p_recv, r_send, r_recv, f_send, f_recv, l_sem,
):
    taps = smoothing_taps()
    t = lax.axis_index("tile")
    x = lax.axis_index("row")
    y = t // (ZS * CS)
    zc = t % (ZS * CS)
    z = zc // CS
    c = zc % CS

    def tile_of(yy, zz, cc):
        return (yy * ZS + zz) * CS + cc

    def device(yy, zz, cc):
        return (tile_of(yy, zz, cc), x)

    z_up, z_down = (z + 1) % ZS, (z + ZS - 1) % ZS
    z_next = (z_up, z_down)
    partner = device(y, z, 1 - c)
    toward = (device(y, z_up, c), device(y, z_down, c))
    y_to = [(y + d) % YS for d in range(YS)]
    y_from = [(y + YS - d) % YS for d in range(YS)]
    x_to = [(x + d) % XS for d in range(XS)]
    x_from = [(x + XS - d) % XS for d in range(XS)]

    load_inten = pltpu.make_async_copy(inten_h, inten, l_sem.at[2])
    load_inten.start()

    barrier = pltpu.get_barrier_semaphore()
    peers = [device(y_to[d], z, c) for d in range(1, YS)]
    peers += [device(y_to[d], zz, c) for d in range(YS) for zz in z_next]
    peers += [(t, x_to[d]) for d in range(1, XS)] + [partner]
    for peer in peers:
        pl.semaphore_signal(barrier, inc=1, device_id=peer, device_id_type=MESH)

    for q in range(YS):
        for r in range(RB):
            vol_s[q, :, r * TV : (r + 1) * TV] = vol[:, q * RB + r, :].astype(BF16)
    pl.semaphore_wait(barrier, len(peers))

    started = []

    def send(src, dst, ssem, rsem, dev):
        copy = pltpu.make_async_remote_copy(
            src_ref=src, dst_ref=dst, send_sem=ssem, recv_sem=rsem,
            device_id=dev, device_id_type=MESH,
        )
        copy.start()
        started.append(copy)

    def arrive(dst, ssem, rsem, dev):
        pltpu.make_async_remote_copy(
            src_ref=dst, dst_ref=dst, send_sem=ssem, recv_sem=rsem,
            device_id=dev, device_id_type=MESH,
        ).wait_recv()

    def y_copy(kind, d, src, dst):
        send(src, dst, y_send.at[kind, d], y_recv.at[kind, d], device(y_to[d], z, c))

    def y_wait(kind, d, dst):
        arrive(dst, y_send.at[kind, d], y_recv.at[kind, d], device(y_from[d], z, c))

    for d in range(YS):
        for way in range(2):
            send(
                vol_s.at[y_to[d]], vol_g.at[y, zc], g_send.at[way, 0, d], g_recv.at[way, 0, d],
                device(y_to[d], z_next[way], c),
            )
    for d in range(1, YS):
        y_copy(0, d, vol_s.at[y_to[d]], vol_g.at[y, zc])
    send(inten_h.at[0, pl.ds(ROWS_HERE - 8, 8), :], halo_lo, h_send.at[0], h_recv.at[0], (t, x_to[1]))
    send(inten_h.at[0, pl.ds(0, 8), :], halo_hi, h_send.at[1], h_recv.at[1], (t, x_from[1]))
    ones = jnp.ones((8, TV), BF16)
    cs_y[y] = dot(ones, foot[0], ((1,), (1,)))
    for d in range(1, YS):
        y_copy(1, d, cs_y.at[y], cs_y.at[y])
    part = pl.ds(pl.multiple_of(x * PART, PART), PART)
    for d in range(1, YS):
        y_copy(2, d, foot.at[0, part], foot_g.at[y, part])
    vol_g[y, zc] = vol_s[y]
    foot_g[y] = foot[0]

    groups = YS * ZS * CS
    member = lax.broadcasted_iota(jnp.int32, (groups, TOTAL), 1)
    owner = lax.broadcasted_iota(jnp.int32, (groups, TOTAL), 0)
    expand = (member // SLOTS == owner).astype(F32).astype(BF16)
    counts = jnp.broadcast_to(count[...].astype(F32), (8, groups)).astype(BF16)
    slot = lax.broadcasted_iota(jnp.int32, (1, TOTAL), 1) % SLOTS
    live = slot.astype(F32) < dot(counts, expand)[0:1]
    block = lax.broadcasted_iota(jnp.int32, (BP, TOTAL), 0)
    offsets = []
    for i in range(YS):
        row = jnp.where(live, off_t[pl.ds(tile_of(i, z, c), 1), :], -1)
        hot[i * BP : (i + 1) * BP, :] = (row == block).astype(F32).astype(BF16)
        offsets.append(row.astype(F32))

    def one_hot_columns():
        rows8 = jnp.concatenate(offsets + [jnp.zeros((8 - YS, TOTAL), F32)], axis=0)
        columns = rows8.T
        block_t = lax.broadcasted_iota(jnp.int32, (TOTAL, CB), 1).astype(F32)
        for i in range(YS):
            hot_t[:, i * CB : (i + 1) * CB] = (columns[:, i : i + 1] == block_t).astype(F32).astype(BF16)
        for h in range(2):
            for i in range(YS):
                back[h, i * CB + BP : (i + 1) * CB, :] = jnp.zeros((CB - BP, SUB), BF16)

    has_lo = (x > 0).astype(F32)
    has_hi = (x < XS - 1).astype(F32)
    lane = lax.broadcasted_iota(jnp.int32, (ROWS_HERE, CB), 1)

    def vertical(b, _):
        cols = pl.ds(pl.multiple_of(b * CB, CB), CB)
        rows_p[b, 0:8, :] = halo_lo[:, cols].astype(F32) * has_lo
        rows_p[b, 8 : 8 + ROWS_HERE, :] = inten[0, :, cols].astype(F32)
        rows_p[b, 8 + ROWS_HERE : 16 + ROWS_HERE, :] = halo_hi[:, cols].astype(F32) * has_hi
        across = taps[RIM] * rows_p[b, 8 : 8 + ROWS_HERE, :]
        for k in range(1, RIM + 1):
            across = across + taps[RIM + k] * (
                rows_p[b, 8 - k : 8 - k + ROWS_HERE, :] + rows_p[b, 8 + k : 8 + k + ROWS_HERE, :]
            )
        rows_a[b + 1] = across
        return 0

    def horizontal(b, _):
        before, here, after = rows_a[b], rows_a[b + 1], rows_a[b + 2]
        smooth = taps[RIM] * here
        for k in range(1, RIM + 1):
            ahead = pltpu.roll(jnp.where(lane < k, after, here), CB - k, 1)
            behind = pltpu.roll(jnp.where(lane >= CB - k, before, here), k, 1)
            smooth = smooth + taps[RIM + k] * (ahead + behind)
        phase = -jnp.log(smooth)
        for q in range(YS):
            ph_s[q, pl.ds(pl.multiple_of(b * RB, RB), RB), :] = phase[q * RB : (q + 1) * RB]
        return 0

    quarter = NCB // 4

    def phase_part(k):
        lax.fori_loop(k * quarter, (k + 1) * quarter, horizontal, 0, unroll=2)
        span = pl.ds(k * quarter * RB, quarter * RB)
        for d in range(1, YS):
            y_copy(6 + k, d, ph_s.at[y_to[d], span], ph.at[y, span])

    def piece(d, zz):
        return vol_g.at[y_from[d], zz * CS + c]

    def give_partner(index, zz):
        src = vol_g.at[:, zz * CS + c]
        send(src, src, q_send.at[index, 0], q_recv.at[index, 0], partner)
        src = cs_g.at[zz * CS + c]
        send(src, src, q_send.at[index, 1], q_recv.at[index, 1], partner)

    def z_far(way, step):
        return (z + ZS - step) % ZS if way == 0 else (z + step) % ZS

    def sums_send(way, step, zz):
        src = cs_g.at[zz * CS + c]
        send(src, src, c_send.at[way, step], c_recv.at[way, step], toward[way])

    def serve(step):
        for d in range(YS):
            for way in range(2):
                if step == 4 and way != d // 2:
                    continue
                zz = z_far(way, step)
                here = piece(d, zz)
                arrive(here, g_send.at[way, step - 1, d], g_recv.at[way, step - 1, d], toward[1 - way])
                if step < 3 or (step == 3 and way == d // 2):
                    send(here, here, g_send.at[way, step, d], g_recv.at[way, step, d], toward[way])
        for way in range(2):
            if step == 4 and way == 1:
                continue
            zz = z_far(way, step)
            arrive(
                cs_g.at[zz * CS + c], c_send.at[way, step - 1], c_recv.at[way, step - 1], toward[1 - way]
            )
            if step < 3 or (step == 3 and way == 0):
                sums_send(way, step, zz)
            give_partner(step if way == 0 else 4 + step, zz)

    rows_a[0] = jnp.zeros((ROWS_HERE, CB), F32)
    rows_a[NCB + 1] = jnp.zeros((ROWS_HERE, CB), F32)
    for d in range(1, YS):
        y_wait(1, d, cs_y.at[y_from[d]])
    cs_g[zc] = cs_y[0] + cs_y[1] + cs_y[2] + cs_y[3]
    for way in range(2):
        sums_send(way, 0, z)
    load_inten.wait()
    arrive(halo_lo, h_send.at[0], h_recv.at[0], (t, x_from[1]))
    arrive(halo_hi, h_send.at[1], h_recv.at[1], (t, x_to[1]))
    lax.fori_loop(0, NCB, vertical, 0, unroll=2)
    serve(1)
    phase_part(0)
    phase_part(1)
    for d in range(1, YS):
        y_wait(0, d, vol_g.at[y_from[d], zc])
    give_partner(0, z)
    for d in range(1, YS):
        y_wait(2, d, foot_g.at[y_from[d], part])
        for e in range(1, XS):
            src = foot_g.at[y_from[d], part]
            send(src, src, x_send.at[d, e], x_recv.at[d, e], (t, x_to[e]))
    phase_part(2)
    phase_part(3)
    ph[y] = ph_s[y]
    serve(2)
    one_hot_columns()
    serve(3)
    serve(4)
    for d in range(1, YS):
        for e in range(1, XS):
            theirs = pl.ds(pl.multiple_of(x_from[e] * PART, PART), PART)
            arrive(foot_g.at[y_from[d], theirs], x_send.at[d, e], x_recv.at[d, e], (t, x_from[e]))
    for index in range(8):
        zz = z_far(0, index) if index < 5 else z_far(1, index - 4)
        arrive(vol_g.at[:, zz * CS + 1 - c], q_send.at[index, 0], q_recv.at[index, 0], partner)
        arrive(cs_g.at[zz * CS + 1 - c], q_send.at[index, 1], q_recv.at[index, 1], partner)

    def load_row(r, _):
        cols = pl.ds(pl.multiple_of(r * TV, TV), TV)
        got = dot(hot[...], vol_g[:, :, :, cols].reshape(TOTAL, TV)).astype(BF16)
        for i in range(YS):
            loads[i, pl.ds(pl.multiple_of(r * BP, BP), BP), :] = got[i * BP : (i + 1) * BP]
        return 0

    lax.fori_loop(0, RB, load_row, 0)

    def image(i, _):
        images[i] = dot(loads[i], foot_g[i])
        return 0

    lax.fori_loop(0, YS, image, 0)
    for k in range(4):
        span = pl.ds(k * quarter * RB, quarter * RB)
        for d in range(1, YS):
            y_wait(6 + k, d, ph.at[y_from[d], span])

    def one_angle(i, _):
        table = foot_g[i]
        counted = jnp.sum(hot[pl.ds(pl.multiple_of(i * BP, BP), BP), :].astype(F32), axis=1, keepdims=True)
        sums = dot(ones, table)[0:1]
        totals = counted * sums[:, :CB] + pltpu.roll(counted * sums[:, CB:], 1, 0)
        scale = (1.0 / jnp.maximum(totals, row_floor))[:NCB]
        for r in range(RB):
            own = images[i, r * BP : (r + 1) * BP, :]
            shadow = own[:, :CB] + pltpu.roll(own[:, CB:], 1, 0)
            left_over = ph[i, pl.ds(r, NCB, stride=RB), :] - shadow[:NCB]
            res_w[i, pl.ds(r, NCB, stride=RB), :] = left_over
            near = jnp.concatenate([left_over * scale, jnp.zeros((BP - NCB, CB), F32)], axis=0)
            far = pltpu.roll(near, BP - 1, 0)
            weigh[r * BP : (r + 1) * BP, :] = jnp.concatenate([near, far], axis=1).astype(BF16)
        spread = dot(weigh[...], table, ((1,), (1,)))
        rows = pl.ds(pl.multiple_of(i * CB, CB), BP)
        for r in range(RB):
            given = spread[r * BP : (r + 1) * BP]
            high = given.astype(BF16)
            back[0, rows, r * TV : (r + 1) * TV] = high
            back[1, rows, r * TV : (r + 1) * TV] = (given - high.astype(F32)).astype(BF16)
        return 0

    lax.fori_loop(0, YS, one_angle, 0)
    for d in range(1, YS):
        y_copy(3, d, res_w.at[y_to[d]], res_out.at[y])
    own_res = pltpu.make_async_copy(res_w.at[y], res_out.at[y], l_sem.at[0])
    own_res.start()

    def term_row(r, _):
        cols = pl.ds(pl.multiple_of(r * TV, TV), TV)
        got = dot(hot_t[...], back[0, :, cols]) + dot(hot_t[...], back[1, :, cols])
        terms[:, :, :, :, cols] = got.reshape(YS, ZS, CS, SLOTS, TV)
        return 0

    halves = [pl.ds(0, SUB // 2), pl.ds(SUB // 2, SUB // 2)]
    for p in range(2):
        lax.fori_loop(p * RB // 2, (p + 1) * RB // 2, term_row, 0)
        for off in (4, 3, 5, 2, 6, 1, 7, 0):
            zz = (z + off) % ZS
            send(
                terms.at[:, zz, 1 - c, :, halves[p]], pair_r.at[zz, :, :, halves[p]],
                p_send.at[off, p], p_recv.at[off, p], partner,
            )

    def add_pair(off, p):
        zz = (z + off) % ZS
        half = halves[p]
        arrive(pair_r.at[zz, :, :, half], p_send.at[off, p], p_recv.at[off, p], partner)
        terms[:, zz, c, :, half] = terms[:, zz, c, :, half] + pair_r[zz, :, :, half]

    for step in range(4):
        for p in range(2):
            for way in range(2):
                off = 4 - step if way == 0 else 4 + step
                half = halves[p]
                if step == 0 and p != way:
                    continue
                add_pair(off, p)
                zz = (z + off) % ZS
                if step > 1 or (step == 1 and p == way):
                    got = ring_r.at[way, step - 1, p]
                    arrive(got, r_send.at[way, step - 1, p], r_recv.at[way, step - 1, p], toward[1 - way])
                    terms[:, zz, c, :, half] = terms[:, zz, c, :, half] + ring_r[way, step - 1, p]
                if step < 3:
                    send(
                        terms.at[:, zz, c, :, half], ring_r.at[way, step, p],
                        r_send.at[way, step, p], r_recv.at[way, step, p], toward[way],
                    )
                    continue
                for d in range(YS):
                    send(
                        terms.at[y_to[d], zz, c, :, half], fin.at[way, y, :, half],
                        f_send.at[way, p, d], f_recv.at[way, p, d], device(y_to[d], zz, c),
                    )
        if step == 1:
            for p in range(2):
                add_pair(0, p)
            for d in range(1, YS):
                y_copy(4, d, terms.at[y_to[d], z, c], fin.at[2, y])
            fin[2, y] = terms[y, z, c]

    total = cs_g[0]
    for k in range(1, ZS * CS):
        total = total + cs_g[k]
    col_out[...] = 1.0 / total
    for d in range(1, YS):
        y_wait(3, d, res_out.at[y_from[d]])
    for d in range(1, YS):
        y_wait(4, d, fin.at[2, y_from[d]])
    for p in range(2):
        for d in range(YS):
            for way in range(2):
                arrive(
                    fin.at[way, y_from[d], :, halves[p]], f_send.at[way, p, d], f_recv.at[way, p, d],
                    device(y_from[d], z_next[1 - way], c),
                )
    for q in range(YS):
        cor_out[q] = fin[0, q] + fin[1, q] + fin[2, q]
    own_res.wait()
    for copy in started:
        copy.wait_send()


def finish(res, cor, col, res_out, cor_out):
    for b in range(NCB):
        res_out[0, :, b * CB : (b + 1) * CB] = res[0, b * RB : (b + 1) * RB, :]
    for r in range(RB):
        cor_out[:, r, :] = cor[0, :, r * TV : (r + 1) * TV] * col[...]


def local(intensity, volume, footprint, foot_offset, tile_count):
    dma = pltpu.SemaphoreType.DMA
    vmem = pl.BlockSpec(memory_space=pltpu.VMEM)
    hbm = pl.BlockSpec(memory_space=pl.ANY)
    residual, summed, columns = pl.pallas_call(
        kernel,
        out_shape=(
            jax.ShapeDtypeStruct((YS, NCB * RB, CB), F32),
            jax.ShapeDtypeStruct((YS, SLOTS, SUB), F32),
            jax.ShapeDtypeStruct((8, TV), F32),
        ),
        in_specs=[hbm] + [vmem] * 4,
        out_specs=(hbm, vmem, vmem),
        scratch_shapes=[
            pltpu.VMEM((1, ROWS_HERE, NCB * CB), BF16),
            pltpu.VMEM((YS, SLOTS, SUB), BF16),
            pltpu.VMEM((YS, ZS * CS, SLOTS, SUB), BF16),
            pltpu.VMEM((YS, TV, TV), BF16),
            pltpu.VMEM((YS, 8, TV), F32),
            pltpu.VMEM((ZS * CS, 8, TV), F32),
            pltpu.VMEM((8, NCB * CB), BF16),
            pltpu.VMEM((8, NCB * CB), BF16),
            pltpu.VMEM((NCB, ROWS_HERE + 16, CB), F32),
            pltpu.VMEM((NCB + 2, ROWS_HERE, CB), F32),
            pltpu.VMEM((YS, NCB * RB, CB), F32),
            pltpu.VMEM((YS, NCB * RB, CB), F32),
            pltpu.VMEM((YS * BP, TOTAL), BF16),
            pltpu.VMEM((TOTAL, YS * CB), BF16),
            pltpu.VMEM((YS, RB * BP, TV), BF16),
            pltpu.VMEM((YS, RB * BP, TV), F32),
            pltpu.VMEM((RB * BP, TV), BF16),
            pltpu.VMEM((YS, NCB * RB, CB), F32),
            pltpu.VMEM((2, YS * CB, SUB), BF16),
            pltpu.VMEM((YS, ZS, CS, SLOTS, SUB), F32),
            pltpu.VMEM((ZS, YS, SLOTS, SUB), F32),
            pltpu.VMEM((2, 3, 2, YS, SLOTS, SUB // 2), F32),
            pltpu.VMEM((3, YS, SLOTS, SUB), F32),
            dma((10, 4)), dma((10, 4)),
            dma((2,)), dma((2,)),
            dma((4, 4)), dma((4, 4)),
            dma((2, 4, 4)), dma((2, 4, 4)),
            dma((2, 4)), dma((2, 4)),
            dma((8, 2)), dma((8, 2)),
            dma((8, 2)), dma((8, 2)),
            dma((2, 3, 2)), dma((2, 3, 2)),
            dma((2, 2, 4)), dma((2, 2, 4)),
            dma((3,)),
        ],
        compiler_params=pltpu.CompilerParams(
            collective_id=0, has_side_effects=True, vmem_limit_bytes=60 << 20
        ),
        name="sirt",
    )(intensity, volume, footprint, foot_offset.T, tile_count.reshape(1, -1))
    return pl.pallas_call(
        finish,
        grid=(YS,),
        out_shape=(
            jax.ShapeDtypeStruct((1, ROWS_HERE, NCB * CB), F32),
            jax.ShapeDtypeStruct((SLOTS, ROWS_HERE, TV), F32),
        ),
        in_specs=[
            pl.BlockSpec((1, NCB * RB, CB), lambda q: (q, 0, 0)),
            pl.BlockSpec((1, SLOTS, SUB), lambda q: (q, 0, 0)),
            pl.BlockSpec((8, TV), lambda q: (0, 0)),
        ],
        out_specs=(
            pl.BlockSpec((1, RB, NCB * CB), lambda q: (0, q, 0)),
            pl.BlockSpec((SLOTS, RB, TV), lambda q: (0, q, 0)),
        ),
        name="finish",
    )(residual, summed, columns)


def solution(mesh):
    placed = (P("tile", "row", None), P("tile", "row", None), P("tile", None, None), P(), P())
    return jax.shard_map(
        local,
        mesh=mesh,
        in_specs=placed,
        out_specs=(P("tile", "row", None), P("tile", "row", None)),
        check_vma=False,
    )
```

time: 92.8 us -> 78.5 us (0.85)
  other arithmetic: 4.96 us -> 0 us
  Pallas kernels: 81.4 us -> 76.7 us
  local copies, waits for them, and re-layouts: 4.18 us -> 0 us
    pallas_call x1, Pallas kernels: 81.4 us -> 73.2 us  [local(): pl.pallas_call(kernel, out_shape=(jax.ShapeDtypeStruct((YS, NCB * RB, CB)...]
    pallas_call x0 -> x1, Pallas kernels: none -> 3.56 us  [local(): pl.pallas_call(finish, grid=(YS,), out_shape=(jax.ShapeDtypeStruct((1, RO...]
    unnamed x1 -> x0, local copies, waits for them, and re-layouts: 2.55 us -> none
    div x1 -> x0, other arithmetic: 1.74 us -> none  [local(): return (residual, summed / columns[0][None, None, :])]
    transpose x1 -> x0, other arithmetic: 1.57 us -> none  [local(): residual, summed, columns = pl.pallas_call(kernel, out_shape=(jax.ShapeDt...]
where the time goes in v2:
time: 78.5 us; the launch traced here: 77.4 us
  Pallas kernels  76.7 us (98%)
    pallas_call x1, Pallas kernels, local(): pl.pallas_call(kernel, out_shape=(jax.ShapeDtypeStruct((YS, NCB * RB, CB)...  73.2 us
    pallas_call x1, Pallas kernels, local(): pl.pallas_call(finish, grid=(YS,), out_shape=(jax.ShapeDtypeStruct((1, RO...  3.56 us

profile of v2, /device:TPU:2, one launch (start us, length us, event | category | flops | bytes accessed | tf_op | source)
XLA Modules:
  0.0 77.4 jit_solution(9864018837161567865)
XLA Ops:
  0.6 73.2 %sirt.1 = (f32[4,704,128]{2,1,0:T(8,128)}, f32[4,8,2048]{2,1,0:T(8,128)}, f32[8,256]{1,0:T(8,128)}) custom-call(bf16[1,32,11264]{2,1,0:T(8,128)(2,1)} %inten_h.1, f32[8,32,256]{2,1,0:T(8,128)} %vol.1, bf16[1,256,256]{2,1,0:T(8,128)(2,1)} %foot.1, s32[64,512]{1,0:T(8,128)} %bitcast.2, s32[1,64]{1,0:T(1,128)} %bitcast.3), custom_call_target="tpu_custom_call" | custom-call | tf_op jit(solution)/shard_map/sirt/pallas_call | solution.py:400
  73.8 3.6 %finish.1 = (f32[1,32,11264]{2,1,0:T(8,128)}, f32[8,32,256]{2,1,0:T(8,128)}) custom-call(f32[4,704,128]{2,1,0:T(8,128)} %get-tuple-element.5.res, f32[4,8,2048]{2,1,0:T(8,128)} %get-tuple-element.6.cor, f32[8,256]{1,0:T(8,128)} %get-tuple-element.7.col), custom_call_target="tpu_custom_call" | custom-call | tf_op jit(solution)/shard_map/finish/pallas_call | solution.py:449

commit v3 on v2

v3 whole, which is shorter than its diff:
```python
import functools

import jax
import jax.numpy as jnp
import numpy as np
from jax import lax
from jax.experimental import pallas as pl
from jax.experimental.pallas import tpu as pltpu
from jax.sharding import PartitionSpec as P

RIM = 3
NCB = 88
CB = 128
TV = 256
YS, ZS, CS, XS = 4, 8, 2, 4
SLOTS = 8
RB = 8
SUB = RB * TV
TOTAL = YS * ZS * CS * SLOTS
BP = 96
PART = TV // XS
HB = RB // 2
HR = NCB * HB
HS = HB * TV
ROWS_HERE = YS * RB

decay_length = 2.0
row_floor = 0.5

F32 = jnp.float32
BF16 = jnp.bfloat16
MESH = pl.DeviceIdType.MESH


def smoothing_taps():
    spread_taps = np.exp(-np.abs(np.arange(-RIM, RIM + 1)) / decay_length)
    return [float(t) for t in (spread_taps / spread_taps.sum()).astype(np.float32)]


def dot(a, b, dims=((1,), (0,))):
    return lax.dot_general(a, b, (dims, ((), ())), preferred_element_type=F32)


def kernel(
    inten_h, vol, foot, off_t, count,
    res_out, cor_out, col_out,
    inten, vol_s, vol_g, foot_g, cs_y, cs_g,
    halo_lo, halo_hi, rows_p, rows_a, ph_s, ph,
    hot, hot_t, loads, images, scale_s, weigh, res_w, back, terms, pair_r, ring_r, fin,
    y_send, y_recv, h_send, h_recv, x_send, x_recv, g_send, g_recv, c_send, c_recv,
    q_send, q_recv, p_send, p_recv, r_send, r_recv, l_sem,
):
    taps = smoothing_taps()
    t = lax.axis_index("tile")
    x = lax.axis_index("row")
    y = t // (ZS * CS)
    zc = t % (ZS * CS)
    z = zc // CS
    c = zc % CS

    def tile_of(yy, zz, cc):
        return (yy * ZS + zz) * CS + cc

    def device(yy, zz, cc):
        return (tile_of(yy, zz, cc), x)

    z_up, z_down = (z + 1) % ZS, (z + ZS - 1) % ZS
    partner = device(y, z, 1 - c)
    toward = (device(y, z_up, c), device(y, z_down, c))
    y_to = [(y + d) % YS for d in range(YS)]
    y_from = [(y + YS - d) % YS for d in range(YS)]
    x_to = [(x + d) % XS for d in range(XS)]
    x_from = [(x + XS - d) % XS for d in range(XS)]

    load_inten = pltpu.make_async_copy(inten_h, inten, l_sem.at[2])
    load_inten.start()

    barrier = pltpu.get_barrier_semaphore()
    peers = [device(y_to[d], z, c) for d in range(1, YS)]
    peers += [device(y, zz, c) for zz in (z_up, z_down)]
    peers += [(t, x_to[d]) for d in range(1, XS)] + [partner]
    for peer in peers:
        pl.semaphore_signal(barrier, inc=1, device_id=peer, device_id_type=MESH)

    for q in range(YS):
        for r in range(RB):
            vol_s[q, :, r * TV : (r + 1) * TV] = vol[:, q * RB + r, :].astype(BF16)
    pl.semaphore_wait(barrier, len(peers))

    started = []

    def send(src, dst, ssem, rsem, dev):
        copy = pltpu.make_async_remote_copy(
            src_ref=src, dst_ref=dst, send_sem=ssem, recv_sem=rsem,
            device_id=dev, device_id_type=MESH,
        )
        copy.start()
        started.append(copy)

    def arrive(dst, ssem, rsem, dev):
        pltpu.make_async_remote_copy(
            src_ref=dst, dst_ref=dst, send_sem=ssem, recv_sem=rsem,
            device_id=dev, device_id_type=MESH,
        ).wait_recv()

    def y_copy(kind, d, src, dst):
        send(src, dst, y_send.at[kind, d], y_recv.at[kind, d], device(y_to[d], z, c))

    def y_wait(kind, d, dst):
        arrive(dst, y_send.at[kind, d], y_recv.at[kind, d], device(y_from[d], z, c))

    halves = [pl.ds(0, HS), pl.ds(HS, HS)]

    for h in range(2):
        for d in range(1, YS):
            y_copy(h, d, vol_s.at[y_to[d], :, halves[h]], vol_g.at[y, zc, :, halves[h]])
    quarter = NCB // 4
    load_inten.wait()
    for k in range(4):
        cols = pl.ds(k * quarter * CB, quarter * CB)
        send(
            inten.at[0, pl.ds(ROWS_HERE - 8, 8), cols], halo_lo.at[:, cols],
            h_send.at[0, k], h_recv.at[0, k], (t, x_to[1]),
        )
        send(inten.at[0, pl.ds(0, 8), cols], halo_hi.at[:, cols], h_send.at[1, k], h_recv.at[1, k], (t, x_from[1]))
    ones = jnp.ones((8, TV), BF16)
    cs_y[y] = dot(ones, foot[0], ((1,), (1,)))
    for d in range(1, YS):
        y_copy(2, d, cs_y.at[y], cs_y.at[y])
    part = pl.ds(pl.multiple_of(x * PART, PART), PART)
    for d in range(1, YS):
        y_copy(3, d, foot.at[0, part], foot_g.at[y, part])
    vol_g[y, zc] = vol_s[y]
    foot_g[y] = foot[0]

    groups = YS * ZS * CS
    member = lax.broadcasted_iota(jnp.int32, (groups, TOTAL), 1)
    owner = lax.broadcasted_iota(jnp.int32, (groups, TOTAL), 0)
    expand = (member // SLOTS == owner).astype(F32).astype(BF16)
    counts = jnp.broadcast_to(count[...].astype(F32), (8, groups)).astype(BF16)
    slot = lax.broadcasted_iota(jnp.int32, (1, TOTAL), 1) % SLOTS
    live = slot.astype(F32) < dot(counts, expand)[0:1]
    block = lax.broadcasted_iota(jnp.int32, (BP, TOTAL), 0)
    offsets = []
    for i in range(YS):
        row = jnp.where(live, off_t[pl.ds(tile_of(i, z, c), 1), :], -1)
        hot[i * BP : (i + 1) * BP, :] = (row == block).astype(F32).astype(BF16)
        offsets.append(row.astype(F32))

    def one_hot_columns():
        rows8 = jnp.concatenate(offsets + [jnp.zeros((8 - YS, TOTAL), F32)], axis=0)
        columns = rows8.T
        block_t = lax.broadcasted_iota(jnp.int32, (TOTAL, CB), 1).astype(F32)
        for i in range(YS):
            hot_t[:, i * CB : (i + 1) * CB] = (columns[:, i : i + 1] == block_t).astype(F32).astype(BF16)
        for h in range(2):
            for i in range(YS):
                back[h, i * CB + BP : (i + 1) * CB, :] = jnp.zeros((CB - BP, SUB), BF16)

    has_lo = (x > 0).astype(F32)
    has_hi = (x < XS - 1).astype(F32)
    lane = lax.broadcasted_iota(jnp.int32, (ROWS_HERE, CB), 1)

    def vertical(b, _):
        cols = pl.ds(pl.multiple_of(b * CB, CB), CB)
        rows_p[b, 0:8, :] = halo_lo[:, cols].astype(F32) * has_lo
        rows_p[b, 8 : 8 + ROWS_HERE, :] = inten[0, :, cols].astype(F32)
        rows_p[b, 8 + ROWS_HERE : 16 + ROWS_HERE, :] = halo_hi[:, cols].astype(F32) * has_hi
        across = taps[RIM] * rows_p[b, 8 : 8 + ROWS_HERE, :]
        for k in range(1, RIM + 1):
            across = across + taps[RIM + k] * (
                rows_p[b, 8 - k : 8 - k + ROWS_HERE, :] + rows_p[b, 8 + k : 8 + k + ROWS_HERE, :]
            )
        rows_a[b + 1] = across
        return 0

    def horizontal(b, _):
        before, here, after = rows_a[b], rows_a[b + 1], rows_a[b + 2]
        smooth = taps[RIM] * here
        for k in range(1, RIM + 1):
            ahead = pltpu.roll(jnp.where(lane < k, after, here), CB - k, 1)
            behind = pltpu.roll(jnp.where(lane >= CB - k, before, here), k, 1)
            smooth = smooth + taps[RIM + k] * (ahead + behind)
        phase = -jnp.log(smooth)
        for q in range(YS):
            for h in range(2):
                first = q * RB + h * HB
                ph_s[q, h, pl.ds(pl.multiple_of(b * HB, HB), HB), :] = phase[first : first + HB]
        return 0

    def smooth_rows(k):
        cols = pl.ds(k * quarter * CB, quarter * CB)
        arrive(halo_lo.at[:, cols], h_send.at[0, k], h_recv.at[0, k], (t, x_from[1]))
        arrive(halo_hi.at[:, cols], h_send.at[1, k], h_recv.at[1, k], (t, x_to[1]))
        lax.fori_loop(k * quarter, (k + 1) * quarter, vertical, 0, unroll=2)

    def phase_part(k):
        lax.fori_loop(k * quarter, (k + 1) * quarter, horizontal, 0, unroll=2)
        span = pl.ds(k * quarter * HB, quarter * HB)
        for d in range(1, YS):
            y_copy(6 + k, d, ph_s.at[y_to[d], 0, span], ph.at[y, 0, span])

    def piece(h, zz, cc):
        return vol_g.at[:, zz * CS + cc, :, halves[h]]

    def give_partner(index, zz, h):
        src = piece(h, zz, c)
        send(src, src, q_send.at[index, h], q_recv.at[index, h], partner)

    def give_partner_sums(index, zz):
        src = cs_g.at[zz * CS + c]
        send(src, src, q_send.at[index, 2], q_recv.at[index, 2], partner)

    def ring_send(way, step, h, zz):
        src = piece(h, zz, c)
        send(src, src, g_send.at[way, step, h], g_recv.at[way, step, h], toward[way])

    def z_far(way, step):
        return (z + ZS - step) % ZS if way == 0 else (z + step) % ZS

    def sums_send(way, step, zz):
        src = cs_g.at[zz * CS + c]
        send(src, src, c_send.at[way, step], c_recv.at[way, step], toward[way])

    def serve(step):
        for h in range(2):
            for way in range(2):
                if step == 4 and way != h:
                    continue
                zz = z_far(way, step)
                arrive(
                    piece(h, zz, c), g_send.at[way, step - 1, h], g_recv.at[way, step - 1, h],
                    toward[1 - way],
                )
                if step < 3 or (step == 3 and way == h):
                    ring_send(way, step, h, zz)
                give_partner(step if way == 0 or step == 4 else 4 + step, zz, h)
        for way in range(2):
            if step == 4 and way == 1:
                continue
            zz = z_far(way, step)
            arrive(
                cs_g.at[zz * CS + c], c_send.at[way, step - 1], c_recv.at[way, step - 1], toward[1 - way]
            )
            if step < 3 or (step == 3 and way == 0):
                sums_send(way, step, zz)
            give_partner_sums(step if way == 0 else 4 + step, zz)

    rows_a[0] = jnp.zeros((ROWS_HERE, CB), F32)
    rows_a[NCB + 1] = jnp.zeros((ROWS_HERE, CB), F32)
    for h in range(2):
        for d in range(1, YS):
            y_wait(h, d, vol_g.at[y_from[d], zc, :, halves[h]])
        for way in range(2):
            ring_send(way, 0, h, z)
        give_partner(0, z, h)
    for d in range(1, YS):
        y_wait(2, d, cs_y.at[y_from[d]])
    cs_g[zc] = cs_y[0] + cs_y[1] + cs_y[2] + cs_y[3]
    for way in range(2):
        sums_send(way, 0, z)
    give_partner_sums(0, z)
    smooth_rows(0)
    smooth_rows(1)
    phase_part(0)
    serve(1)
    smooth_rows(2)
    phase_part(1)
    smooth_rows(3)
    phase_part(2)
    serve(2)
    phase_part(3)
    for d in range(1, YS):
        y_copy(4, d, ph_s.at[y_to[d], 1], ph.at[y, 1])
    ph[y] = ph_s[y]
    for d in range(1, YS):
        y_wait(3, d, foot_g.at[y_from[d], part])
        for e in range(1, XS):
            src = foot_g.at[y_from[d], part]
            send(src, src, x_send.at[d, e], x_recv.at[d, e], (t, x_to[e]))
    serve(3)
    one_hot_columns()
    for d in range(1, YS):
        for e in range(1, XS):
            theirs = pl.ds(pl.multiple_of(x_from[e] * PART, PART), PART)
            arrive(foot_g.at[y_from[d], theirs], x_send.at[d, e], x_recv.at[d, e], (t, x_from[e]))
    serve(4)

    def take_partner(h):
        for index in range(8):
            zz = z_far(0, index) if index < 5 else z_far(1, index - 4)
            arrive(piece(h, zz, 1 - c), q_send.at[index, h], q_recv.at[index, h], partner)
            if h == 1:
                arrive(cs_g.at[zz * CS + 1 - c], q_send.at[index, 2], q_recv.at[index, 2], partner)

    def scales(i, _):
        counted = jnp.sum(hot[pl.ds(pl.multiple_of(i * BP, BP), BP), :].astype(F32), axis=1, keepdims=True)
        sums = dot(ones, foot_g[i])[0:1]
        totals = counted * sums[:, :CB] + pltpu.roll(counted * sums[:, CB:], 1, 0)
        scale_s[i] = 1.0 / jnp.maximum(totals, row_floor)
        return 0

    lax.fori_loop(0, YS, scales, 0)

    def shadows(h):
        take_partner(h)

        def load_row(r, _):
            cols = pl.ds(pl.multiple_of((h * HB + r) * TV, TV), TV)
            got = dot(hot[...], vol_g[:, :, :, cols].reshape(TOTAL, TV)).astype(BF16)
            for i in range(YS):
                loads[i, pl.ds(pl.multiple_of(r * BP, BP), BP), :] = got[i * BP : (i + 1) * BP]
            return 0

        lax.fori_loop(0, HB, load_row, 0)

        def image(i, _):
            images[h, i] = dot(loads[i], foot_g[i])
            return 0

        lax.fori_loop(0, YS, image, 0)

    def weights(h):
        if h == 0:
            for k in range(4):
                span = pl.ds(k * quarter * HB, quarter * HB)
                for d in range(1, YS):
                    y_wait(6 + k, d, ph.at[y_from[d], 0, span])
        else:
            for d in range(1, YS):
                y_wait(4, d, ph.at[y_from[d], 1])

        def one_angle(i, _):
            scale = scale_s[i, :NCB, :]
            for r in range(HB):
                own = images[h, i, r * BP : (r + 1) * BP, :]
                shadow = own[:, :CB] + pltpu.roll(own[:, CB:], 1, 0)
                left_over = ph[i, h, pl.ds(r, NCB, stride=HB), :] - shadow[:NCB]
                res_w[i, h, pl.ds(r, NCB, stride=HB), :] = left_over
                near = jnp.concatenate([left_over * scale, jnp.zeros((BP - NCB, CB), F32)], axis=0)
                far = pltpu.roll(near, BP - 1, 0)
                weigh[r * BP : (r + 1) * BP, :] = jnp.concatenate([near, far], axis=1).astype(BF16)
            spread = dot(weigh[...], foot_g[i], ((1,), (1,)))
            rows = pl.ds(pl.multiple_of(i * CB, CB), BP)
            for r in range(HB):
                given = spread[r * BP : (r + 1) * BP]
                high = given.astype(BF16)
                cols = pl.ds((h * HB + r) * TV, TV)
                back[0, rows, cols] = high
                back[1, rows, cols] = (given - high.astype(F32)).astype(BF16)
            return 0

        lax.fori_loop(0, YS, one_angle, 0)
        for d in range(1, YS):
            y_copy(10 + h, d, res_w.at[y_to[d], h], res_out.at[y, h])
        pltpu.make_async_copy(res_w.at[y, h], res_out.at[y, h], l_sem.at[h]).start()

    def sums_of(h):
        def term_row(r, _):
            cols = pl.ds(pl.multiple_of(r * TV, TV), TV)
            got = dot(hot_t[...], back[0, :, cols]) + dot(hot_t[...], back[1, :, cols])
            terms[:, :, :, :, cols] = got.reshape(YS, ZS, CS, SLOTS, TV)
            return 0

        lax.fori_loop(h * HB, (h + 1) * HB, term_row, 0)
        for off in (4, 3, 5, 2, 6, 1, 7, 0):
            zz = (z + off) % ZS
            send(
                terms.at[:, zz, 1 - c, :, halves[h]], pair_r.at[h, zz],
                p_send.at[off, h], p_recv.at[off, h], partner,
            )

    def add_pair(off, h):
        zz = (z + off) % ZS
        arrive(pair_r.at[h, zz], p_send.at[off, h], p_recv.at[off, h], partner)
        terms[:, zz, c, :, halves[h]] = terms[:, zz, c, :, halves[h]] + pair_r[h, zz]

    def add_ring(way, step, h, p, zz):
        got = ring_r.at[h, way, step, p]
        arrive(got, r_send.at[h, way, step, p], r_recv.at[h, way, step, p], toward[1 - way])
        ys = pl.ds(2 * p, 2)
        terms[ys, zz, c, :, halves[h]] = terms[ys, zz, c, :, halves[h]] + ring_r[h, way, step, p]

    def sum_step(h, step):
        for way in range(2):
            if step > 0 or way == 0:
                add_pair(4 - step if way == 0 else 4 + step, h)
        for p in range(2):
            for way in range(2):
                if step == 0 and p != way:
                    continue
                zz = (z + 4 - step) % ZS if way == 0 else (z + 4 + step) % ZS
                if step > 1 or (step == 1 and p == way):
                    add_ring(way, step - 1, h, p, zz)
                send(
                    terms.at[pl.ds(2 * p, 2), zz, c, :, halves[h]], ring_r.at[h, way, step, p],
                    r_send.at[h, way, step, p], r_recv.at[h, way, step, p], toward[way],
                )
        if step == 2:
            add_pair(0, h)

    def sum_end(h):
        for p in range(2):
            for way in range(2):
                add_ring(way, 3, h, p, z)
        for d in range(1, YS):
            y_copy(12 + h, d, terms.at[y_to[d], z, c, :, halves[h]], fin.at[h, y])
        fin[h, y] = terms[y, z, c, :, halves[h]]

    shadows(0)
    weights(0)
    sums_of(0)
    sum_step(0, 0)
    shadows(1)
    sum_step(0, 1)
    weights(1)
    sums_of(1)
    sum_step(0, 2)
    sum_step(1, 0)
    sum_step(0, 3)
    sum_step(1, 1)
    sum_step(1, 2)
    sum_end(0)
    sum_step(1, 3)
    total = cs_g[0]
    for k in range(1, ZS * CS):
        total = total + cs_g[k]
    col_out[...] = 1.0 / total
    sum_end(1)
    for h in range(2):
        for d in range(1, YS):
            y_wait(10 + h, d, res_out.at[y_from[d], h])
        for d in range(1, YS):
            y_wait(12 + h, d, fin.at[h, y_from[d]])
        cor_out[h] = fin[h]
        pltpu.make_async_copy(res_w.at[y, h], res_out.at[y, h], l_sem.at[h]).wait()
    for copy in started:
        copy.wait_send()


def finish(res, cor, col, res_out, cor_out):
    for h in range(2):
        for b in range(NCB):
            res_out[0, h * HB : (h + 1) * HB, b * CB : (b + 1) * CB] = res[0, h, b * HB : (b + 1) * HB, :]
        for r in range(HB):
            cor_out[:, h * HB + r, :] = cor[h, 0, :, r * TV : (r + 1) * TV] * col[...]


def local(intensity, volume, footprint, foot_offset, tile_count):
    dma = pltpu.SemaphoreType.DMA
    vmem = pl.BlockSpec(memory_space=pltpu.VMEM)
    hbm = pl.BlockSpec(memory_space=pl.ANY)
    residual, summed, columns = pl.pallas_call(
        kernel,
        out_shape=(
            jax.ShapeDtypeStruct((YS, 2, HR, CB), F32),
            jax.ShapeDtypeStruct((2, YS, SLOTS, HS), F32),
            jax.ShapeDtypeStruct((8, TV), F32),
        ),
        in_specs=[hbm] + [vmem] * 4,
        out_specs=(hbm, vmem, vmem),
        scratch_shapes=[
            pltpu.VMEM((1, ROWS_HERE, NCB * CB), BF16),
            pltpu.VMEM((YS, SLOTS, SUB), BF16),
            pltpu.VMEM((YS, ZS * CS, SLOTS, SUB), BF16),
            pltpu.VMEM((YS, TV, TV), BF16),
            pltpu.VMEM((YS, 8, TV), F32),
            pltpu.VMEM((ZS * CS, 8, TV), F32),
            pltpu.VMEM((8, NCB * CB), BF16),
            pltpu.VMEM((8, NCB * CB), BF16),
            pltpu.VMEM((NCB, ROWS_HERE + 16, CB), F32),
            pltpu.VMEM((NCB + 2, ROWS_HERE, CB), F32),
            pltpu.VMEM((YS, 2, HR, CB), F32),
            pltpu.VMEM((YS, 2, HR, CB), F32),
            pltpu.VMEM((YS * BP, TOTAL), BF16),
            pltpu.VMEM((TOTAL, YS * CB), BF16),
            pltpu.VMEM((YS, HB * BP, TV), BF16),
            pltpu.VMEM((2, YS, HB * BP, TV), F32),
            pltpu.VMEM((YS, BP, CB), F32),
            pltpu.VMEM((HB * BP, TV), BF16),
            pltpu.VMEM((YS, 2, HR, CB), F32),
            pltpu.VMEM((2, YS * CB, SUB), BF16),
            pltpu.VMEM((YS, ZS, CS, SLOTS, SUB), F32),
            pltpu.VMEM((2, ZS, YS, SLOTS, HS), F32),
            pltpu.VMEM((2, 2, 4, 2, 2, SLOTS, HS), F32),
            pltpu.VMEM((2, YS, SLOTS, HS), F32),
            dma((14, 4)), dma((14, 4)),
            dma((2, 4)), dma((2, 4)),
            dma((4, 4)), dma((4, 4)),
            dma((2, 4, 2)), dma((2, 4, 2)),
            dma((2, 4)), dma((2, 4)),
            dma((8, 3)), dma((8, 3)),
            dma((8, 2)), dma((8, 2)),
            dma((2, 2, 4, 2)), dma((2, 2, 4, 2)),
            dma((3,)),
        ],
        compiler_params=pltpu.CompilerParams(
            collective_id=0, has_side_effects=True, vmem_limit_bytes=60 << 20
        ),
        name="sirt",
    )(intensity, volume, footprint, foot_offset.T, tile_count.reshape(1, -1))
    return pl.pallas_call(
        finish,
        grid=(YS,),
        out_shape=(
            jax.ShapeDtypeStruct((1, ROWS_HERE, NCB * CB), F32),
            jax.ShapeDtypeStruct((SLOTS, ROWS_HERE, TV), F32),
        ),
        in_specs=[
            pl.BlockSpec((1, 2, HR, CB), lambda q: (q, 0, 0, 0)),
            pl.BlockSpec((2, 1, SLOTS, HS), lambda q: (0, q, 0, 0)),
            pl.BlockSpec((8, TV), lambda q: (0, 0)),
        ],
        out_specs=(
            pl.BlockSpec((1, RB, NCB * CB), lambda q: (0, q, 0)),
            pl.BlockSpec((SLOTS, RB, TV), lambda q: (0, q, 0)),
        ),
        name="finish",
    )(residual, summed, columns)


def solution(mesh):
    placed = (P("tile", "row", None), P("tile", "row", None), P("tile", None, None), P(), P())
    return jax.shard_map(
        local,
        mesh=mesh,
        in_specs=placed,
        out_specs=(P("tile", "row", None), P("tile", "row", None)),
        check_vma=False,
    )
```

time: 78.5 us -> 77.4 us (0.986); the launches traced: 77.4 us -> 77.2 us
  no operation moved by 1% of the time
where the time goes in v3:
time: 77.4 us; the launch traced here: 77.2 us
  Pallas kernels  76.5 us (99%)
    pallas_call x1, Pallas kernels, local(): pl.pallas_call(kernel, out_shape=(jax.ShapeDtypeStruct((YS, 2, HR, CB), F...  72.8 us
    pallas_call x1, Pallas kernels, local(): pl.pallas_call(finish, grid=(YS,), out_shape=(jax.ShapeDtypeStruct((1, RO...  3.69 us

profile of v3, /device:TPU:2, one launch (start us, length us, event | category | flops | bytes accessed | tf_op | source)
XLA Modules:
  0.0 77.2 jit_solution(7138153739951130797)
XLA Ops:
  0.6 72.8 %sirt.1 = (f32[4,2,352,128]{3,2,1,0:T(8,128)}, f32[2,4,8,1024]{3,2,1,0:T(8,128)}, f32[8,256]{1,0:T(8,128)}) custom-call(bf16[1,32,11264]{2,1,0:T(8,128)(2,1)} %inten_h.1, f32[8,32,256]{2,1,0:T(8,128)} %vol.1, bf16[1,256,256]{2,1,0:T(8,128)(2,1)} %foot.1, s32[64,512]{1,0:T(8,128)} %bitcast.2, s32[1,64]{1,0:T(1,128)} %bitcast.3), custom_call_target="tpu_custom_call" | custom-call | tf_op jit(solution)/shard_map/sirt/pallas_call | solution.py:453
  73.5 3.7 %finish.1 = (f32[1,32,11264]{2,1,0:T(8,128)}, f32[8,32,256]{2,1,0:T(8,128)}) custom-call(f32[4,2,352,128]{3,2,1,0:T(8,128)} %get-tuple-element.5.res, f32[2,4,8,1024]{3,2,1,0:T(8,128)} %get-tuple-element.6.cor, f32[8,256]{1,0:T(8,128)} %get-tuple-element.7.col), custom_call_target="tpu_custom_call" | custom-call | tf_op jit(solution)/shard_map/finish/pallas_call | solution.py:502

commit v4 on v3

--- a/solution.py
+++ b/solution.py
@@ -195,7 +195,7 @@
         lax.fori_loop(k * quarter, (k + 1) * quarter, vertical, 0, unroll=2)
 
     def phase_part(k):
-        lax.fori_loop(k * quarter, (k + 1) * quarter, horizontal, 0, unroll=2)
+        lax.fori_loop(k * quarter, (k + 1) * quarter, horizontal, 0, unroll=11)
         span = pl.ds(k * quarter * HB, quarter * HB)
         for d in range(1, YS):
             y_copy(6 + k, d, ph_s.at[y_to[d], 0, span], ph.at[y, 0, span])
@@ -211,9 +211,12 @@
         src = cs_g.at[zz * CS + c]
         send(src, src, q_send.at[index, 2], q_recv.at[index, 2], partner)
 
-    def ring_send(way, step, h, zz):
-        src = piece(h, zz, c)
-        send(src, src, g_send.at[way, step, h], g_recv.at[way, step, h], toward[way])
+    def ring_piece(h, p, zz):
+        return vol_g.at[pl.ds(2 * p, 2), zz * CS + c, :, halves[h]]
+
+    def ring_send(way, step, h, p, zz):
+        src = ring_piece(h, p, zz)
+        send(src, src, g_send.at[way, step, h, p], g_recv.at[way, step, h, p], toward[way])
 
     def z_far(way, step):
         return (z + ZS - step) % ZS if way == 0 else (z + step) % ZS
@@ -224,17 +227,19 @@
 
     def serve(step):
         for h in range(2):
-            for way in range(2):
-                if step == 4 and way != h:
-                    continue
-                zz = z_far(way, step)
-                arrive(
-                    piece(h, zz, c), g_send.at[way, step - 1, h], g_recv.at[way, step - 1, h],
-                    toward[1 - way],
-                )
-                if step < 3 or (step == 3 and way == h):
-                    ring_send(way, step, h, zz)
-                give_partner(step if way == 0 or step == 4 else 4 + step, zz, h)
+            for p in range(2):
+                for way in range(2):
+                    if step == 4 and way != p:
+                        continue
+                    zz = z_far(way, step)
+                    arrive(
+                        ring_piece(h, p, zz), g_send.at[way, step - 1, h, p],
+                        g_recv.at[way, step - 1, h, p], toward[1 - way],
+                    )
+                    if step < 3 or (step == 3 and way == p):
+                        ring_send(way, step, h, p, zz)
+            for way in range(2 if step < 4 else 1):
+                give_partner(step if way == 0 else 4 + step, z_far(way, step), h)
         for way in range(2):
             if step == 4 and way == 1:
                 continue
@@ -251,8 +256,9 @@
     for h in range(2):
         for d in range(1, YS):
             y_wait(h, d, vol_g.at[y_from[d], zc, :, halves[h]])
-        for way in range(2):
-            ring_send(way, 0, h, z)
+        for p in range(2):
+            for way in range(2):
+                ring_send(way, 0, h, p, z)
         give_partner(0, z, h)
     for d in range(1, YS):
         y_wait(2, d, cs_y.at[y_from[d]])
@@ -375,36 +381,38 @@
         arrive(pair_r.at[h, zz], p_send.at[off, h], p_recv.at[off, h], partner)
         terms[:, zz, c, :, halves[h]] = terms[:, zz, c, :, halves[h]] + pair_r[h, zz]
 
-    def add_ring(way, step, h, p, zz):
-        got = ring_r.at[h, way, step, p]
-        arrive(got, r_send.at[h, way, step, p], r_recv.at[h, way, step, p], toward[1 - way])
-        ys = pl.ds(2 * p, 2)
-        terms[ys, zz, c, :, halves[h]] = terms[ys, zz, c, :, halves[h]] + ring_r[h, way, step, p]
+    def add_ring(way, step, h, d, zz):
+        got = ring_r.at[h, way, step, d]
+        arrive(got, r_send.at[h, way, step, d], r_recv.at[h, way, step, d], toward[1 - way])
+        mine = y_to[d]
+        terms[mine, zz, c, :, halves[h]] = terms[mine, zz, c, :, halves[h]] + ring_r[h, way, step, d]
 
     def sum_step(h, step):
         for way in range(2):
             if step > 0 or way == 0:
                 add_pair(4 - step if way == 0 else 4 + step, h)
-        for p in range(2):
+        for e in range(2):
             for way in range(2):
-                if step == 0 and p != way:
-                    continue
-                zz = (z + 4 - step) % ZS if way == 0 else (z + 4 + step) % ZS
-                if step > 1 or (step == 1 and p == way):
-                    add_ring(way, step - 1, h, p, zz)
-                send(
-                    terms.at[pl.ds(2 * p, 2), zz, c, :, halves[h]], ring_r.at[h, way, step, p],
-                    r_send.at[h, way, step, p], r_recv.at[h, way, step, p], toward[way],
-                )
+                for p in range(2):
+                    if step == 0 and p != way:
+                        continue
+                    d = 2 * p + e
+                    zz = (z + 4 - step) % ZS if way == 0 else (z + 4 + step) % ZS
+                    if step > 1 or (step == 1 and p == way):
+                        add_ring(way, step - 1, h, d, zz)
+                    send(
+                        terms.at[y_to[d], zz, c, :, halves[h]], ring_r.at[h, way, step, d],
+                        r_send.at[h, way, step, d], r_recv.at[h, way, step, d], toward[way],
+                    )
         if step == 2:
             add_pair(0, h)
 
     def sum_end(h):
-        for p in range(2):
+        for d in (2, 1, 3, 0):
             for way in range(2):
-                add_ring(way, 3, h, p, z)
-        for d in range(1, YS):
-            y_copy(12 + h, d, terms.at[y_to[d], z, c, :, halves[h]], fin.at[h, y])
+                add_ring(way, 3, h, d, z)
+            if d > 0:
+                y_copy(12 + h, d, terms.at[y_to[d], z, c, :, halves[h]], fin.at[h, y])
         fin[h, y] = terms[y, z, c, :, halves[h]]
 
     shadows(0)
@@ -482,16 +490,16 @@
             pltpu.VMEM((2, YS * CB, SUB), BF16),
             pltpu.VMEM((YS, ZS, CS, SLOTS, SUB), F32),
             pltpu.VMEM((2, ZS, YS, SLOTS, HS), F32),
-            pltpu.VMEM((2, 2, 4, 2, 2, SLOTS, HS), F32),
+            pltpu.VMEM((2, 2, 4, YS, SLOTS, HS), F32),
             pltpu.VMEM((2, YS, SLOTS, HS), F32),
             dma((14, 4)), dma((14, 4)),
             dma((2, 4)), dma((2, 4)),
             dma((4, 4)), dma((4, 4)),
-            dma((2, 4, 2)), dma((2, 4, 2)),
+            dma((2, 4, 2, 2)), dma((2, 4, 2, 2)),
             dma((2, 4)), dma((2, 4)),
             dma((8, 3)), dma((8, 3)),
             dma((8, 2)), dma((8, 2)),
-            dma((2, 2, 4, 2)), dma((2, 2, 4, 2)),
+            dma((2, 2, 4, 4)), dma((2, 2, 4, 4)),
             dma((3,)),
         ],
         compiler_params=pltpu.CompilerParams(

time: 77.4 us -> 74.9 us (0.968)
  Pallas kernels: 76.5 us -> 74.1 us
    pallas_call x1, Pallas kernels: 72.8 us -> 70.4 us  [local(): pl.pallas_call(kernel, out_shape=(jax.ShapeDtypeStruct((YS, 2, HR, CB), F...]
where the time goes in v4:
time: 74.9 us; the launch traced here: 74.7 us
  Pallas kernels  74.1 us (99%)
    pallas_call x1, Pallas kernels, local(): pl.pallas_call(kernel, out_shape=(jax.ShapeDtypeStruct((YS, 2, HR, CB), F...  70.4 us
    pallas_call x1, Pallas kernels, local(): pl.pallas_call(finish, grid=(YS,), out_shape=(jax.ShapeDtypeStruct((1, RO...  3.69 us

profile of v4, /device:TPU:2, one launch (start us, length us, event | category | flops | bytes accessed | tf_op | source)
XLA Modules:
  0.0 74.7 jit_solution(710098819232529674)
XLA Ops:
  0.6 70.4 %sirt.1 = (f32[4,2,352,128]{3,2,1,0:T(8,128)}, f32[2,4,8,1024]{3,2,1,0:T(8,128)}, f32[8,256]{1,0:T(8,128)}) custom-call(bf16[1,32,11264]{2,1,0:T(8,128)(2,1)} %inten_h.1, f32[8,32,256]{2,1,0:T(8,128)} %vol.1, bf16[1,256,256]{2,1,0:T(8,128)(2,1)} %foot.1, s32[64,512]{1,0:T(8,128)} %bitcast.2, s32[1,64]{1,0:T(1,128)} %bitcast.3), custom_call_target="tpu_custom_call" | custom-call | tf_op jit(solution)/shard_map/sirt/pallas_call | solution.py:461
  71.0 3.7 %finish.1 = (f32[1,32,11264]{2,1,0:T(8,128)}, f32[8,32,256]{2,1,0:T(8,128)}) custom-call(f32[4,2,352,128]{3,2,1,0:T(8,128)} %get-tuple-element.5.res, f32[2,4,8,1024]{3,2,1,0:T(8,128)} %get-tuple-element.6.cor, f32[8,256]{1,0:T(8,128)} %get-tuple-element.7.col), custom_call_target="tpu_custom_call" | custom-call | tf_op jit(solution)/shard_map/finish/pallas_call | solution.py:510

commit v5 on v4

--- a/solution.py
+++ b/solution.py
@@ -420,13 +420,13 @@
     sums_of(0)
     sum_step(0, 0)
     shadows(1)
-    sum_step(0, 1)
     weights(1)
     sums_of(1)
+    sum_step(0, 1)
+    sum_step(1, 0)
     sum_step(0, 2)
-    sum_step(1, 0)
+    sum_step(1, 1)
     sum_step(0, 3)
-    sum_step(1, 1)
     sum_step(1, 2)
     sum_end(0)
     sum_step(1, 3)

time: 74.9 us -> 74.3 us (level)
  no operation moved by 1% of the time
where the time goes in v5:
time: 74.3 us; the launch traced here: 74.1 us
  Pallas kernels  73.5 us (99%)
    pallas_call x1, Pallas kernels, local(): pl.pallas_call(kernel, out_shape=(jax.ShapeDtypeStruct((YS, 2, HR, CB), F...  69.8 us
    pallas_call x1, Pallas kernels, local(): pl.pallas_call(finish, grid=(YS,), out_shape=(jax.ShapeDtypeStruct((1, RO...  3.69 us

profile of v5, /device:TPU:2, one launch (start us, length us, event | category | flops | bytes accessed | tf_op | source)
XLA Modules:
  0.0 74.1 jit_solution(13408328698284031943)
XLA Ops:
  0.6 69.8 %sirt.1 = (f32[4,2,352,128]{3,2,1,0:T(8,128)}, f32[2,4,8,1024]{3,2,1,0:T(8,128)}, f32[8,256]{1,0:T(8,128)}) custom-call(bf16[1,32,11264]{2,1,0:T(8,128)(2,1)} %inten_h.1, f32[8,32,256]{2,1,0:T(8,128)} %vol.1, bf16[1,256,256]{2,1,0:T(8,128)(2,1)} %foot.1, s32[64,512]{1,0:T(8,128)} %bitcast.2, s32[1,64]{1,0:T(1,128)} %bitcast.3), custom_call_target="tpu_custom_call" | custom-call | tf_op jit(solution)/shard_map/sirt/pallas_call | solution.py:461
  70.4 3.7 %finish.1 = (f32[1,32,11264]{2,1,0:T(8,128)}, f32[8,32,256]{2,1,0:T(8,128)}) custom-call(f32[4,2,352,128]{3,2,1,0:T(8,128)} %get-tuple-element.5.res, f32[2,4,8,1024]{3,2,1,0:T(8,128)} %get-tuple-element.6.cor, f32[8,256]{1,0:T(8,128)} %get-tuple-element.7.col), custom_call_target="tpu_custom_call" | custom-call | tf_op jit(solution)/shard_map/finish/pallas_call | solution.py:510
